TPU v7x, 16 devices: a 4x2x1 block of a 4x4x8 slice. The times are simulated.
16 devices in a mesh: dp: 2 (over y, z), tp: 8 (over x, core).
Axes of the slice: x: 4, y: 2, z: 1, core: 2. Of those that a mesh axis runs over, the one named last changes fastest.
The devices are a block of a 4x4x8 slice.
Arguments:
- x_in: bfloat16 [512, 3584], P(('dp', 'tp')), parts along dimension 0
- w_in: bfloat16 [3584, 18944], P(None, 'tp')
- grad_out: bfloat16 [512, 18944], P('dp', 'tp'), parts along dimension 0
Outputs:
- output 1: bfloat16 [512, 3584], P(('dp', 'tp')), parts along dimension 0
- output 2: float32 [7168, 18944], P('dp', 'tp'), parts along dimension 0
There are 2 independent parts. A program takes and returns all parts, laid end to end along the dimension named above; an argument that names none is the same for every part.
All inputs are finite; a program needn't handle non-finite values.
Results may differ from a plain program's by a relative error of at most 0.001.
Values are sent between devices in bfloat16 or wider.
A program may use at most 768 MiB of HBM per device.

v0:
```python
import jax
import jax.numpy as jnp
from jax import lax
from jax.sharding import PartitionSpec as P


def solution(mesh):
    def per_device(x_blk, w_blk, grad_blk):
        x_full = lax.all_gather(x_blk, "tp", axis=0, tiled=True)
        part_dx = lax.dot_general(grad_blk, w_blk, (((1,), (1,)), ((), ())), preferred_element_type=jnp.float32)
        grad_x = lax.psum_scatter(part_dx, "tp", scatter_dimension=0, tiled=True).astype(jnp.bfloat16)
        grad_w = lax.dot_general(x_full, grad_blk, (((0,), (0,)), ((), ())), preferred_element_type=jnp.float32)
        return grad_x, grad_w

    return jax.shard_map(
        per_device,
        mesh=mesh,
        in_specs=(P(("dp", "tp"), None), P(None, "tp"), P("dp", "tp")),
        out_specs=(P(("dp", "tp"), None), P("dp", "tp")),
        check_vma=False,
    )
```

profile of v0, /device:TPU:112, one launch (start us, length us, event | category | flops | bytes accessed | tf_op | source)
XLA Modules:
  0.0 77.2 jit_solution(3457094261120325739)
XLA Ops:
  7.2 0.0 copy-start
  7.2 0.1 all-gather.2.cloned.1.call-start
  7.3 0.7 all-gather.2.cloned.1.call-update
  8.0 0.1 reduce-scatter.2.cloned.1.call-start
  8.1 0.4 copy-done
  8.5 10.4 %fusion = f32[256,3584]{1,0:T(8,128)} fusion(bf16[256,2368]{0,1:T(8,128)(2,1)S(1)} %copy-done, bf16[3584,2368]{0,1:T(8,128)(2,1)} %param.4), kind=kOutput, calls=%fused_computation | convolution fusion | flops 4345298944 | bytes 21856256 | tf_op jit(solution)/shard_map/dot_general | solution.py:10
  18.8 0.1 reduce-scatter.2.cloned.1.call-update
  18.9 14.2 %all-gather.2.cloned.1.call-done = bf16[256,3584]{1,0:T(8,128)(2,1)} async-done(((bf16[32,3584]{1,0:T(8,128)(2,1)}), bf16[256,3584]{1,0:T(8,128)(2,1)}) %all-gather.2.cloned.1.call-update) | async-done | bytes 1835024 | tf_op jit(solution)/shard_map/all_gather | solution.py:9
  33.1 15.7 %fusion.1 = f32[3584,2368]{0,1:T(8,128)} fusion(bf16[256,2368]{0,1:T(8,128)(2,1)S(1)} %copy-done, bf16[256,3584]{1,0:T(8,128)(2,1)} %all-gather.2.cloned.1.call-done), kind=kOutput, calls=%fused_computation.1 | convolution fusion | flops 4345298944 | bytes 36995072 | tf_op jit(solution)/shard_map/dot_general | solution.py:12
  48.8 19.8 %reduce-scatter.2.cloned.1.call-done = f32[32,3584]{1,0:T(8,128)} async-done(((f32[256,3584]{1,0:T(8,128)}), f32[32,3584]{1,0:T(8,128)}) %reduce-scatter.2.cloned.1.call-update) | async-done | bytes 458768 | tf_op jit(solution)/shard_map/reduce_scatter | solution.py:11
  68.6 1.7 %convert_element_type.3 = bf16[32,3584]{1,0:T(8,128)(2,1)} convert(f32[32,3584]{1,0:T(8,128)} %reduce-scatter.2.cloned.1.call-done) | non-fusion elementwise | flops 114688 | bytes 688128 | tf_op jit(solution)/shard_map/convert_element_type | solution.py:11
Async XLA Ops:
  7.2 1.3 %copy-start = (bf16[256,2368]{0,1:T(8,128)(2,1)S(1)}, bf16[256,2368]{0,1:T(8,128)(2,1)}, u32[]{:S(2)}) copy-start(bf16[256,2368]{0,1:T(8,128)(2,1)} %param.5) | copy-start | bytes 3637252
  7.2 25.9 %all-gather.2.cloned.1.call-start = ((), (), s32[]{:S(2)}) async-start(), calls=%async_computation.2 | async-start | bytes 2064384 | tf_op jit(solution)/shard_map/all_gather | solution.py:9
  8.0 60.6 %reduce-scatter.2.cloned.1.call-start = ((), (), s32[]{:S(2)}) async-start(), calls=%async_computation.1 | async-start | bytes 4128768 | tf_op jit(solution)/shard_map/reduce_scatter | solution.py:11
Sparse Core Ops, SparseCore 0:
  9.6 23.4 all-gather.1
  35.4 33.1 reduce-scatter.1
where the time goes:
time: 77.4 us; the launch traced here: 77.2 us
  waiting for transfers between devices  34.8 us (45%)
  matrix products  26 us (34%)
  between operations  14.1 us (18%)
  other arithmetic  1.73 us (2%)
    reduce_scatter x1, waiting for transfers between devices, per_device(): lax.psum_scatter(part_dx, 'tp', scatter_dimension=0, tiled=True)  19.8 us
    dot_general x1, matrix products, per_device(): lax.dot_general(x_full, grad_blk, (((0,), (0,)), ((), ())), preferred_ele...  15.7 us
    all_gather x1, waiting for transfers between devices, per_device(): x_full = lax.all_gather(x_blk, 'tp', axis=0, tiled=True)  14.2 us
    dot_general x1, matrix products, per_device(): lax.dot_general(grad_blk, w_blk, (((1,), (1,)), ((), ())), preferred_elem...  10.4 us
    convert_element_type x1, other arithmetic, per_device(): lax.psum_scatter(part_dx, 'tp', scatter_dimension=0, tiled=True)  1.73 us
  transfers between devices with their start and end apart: 2, of which 2 were waited for; matrix products, arithmetic and copies ran while one was open for 34% of the time, Pallas kernels for 0%

commit v1 on v0

v1 whole, which is shorter than its diff:
```python
import functools

import jax
import jax.numpy as jnp
from jax import lax
from jax.experimental import pallas as pl
from jax.experimental.pallas import tpu as pltpu
from jax.sharding import PartitionSpec as P

MESH = pl.DeviceIdType.MESH
F32 = jnp.float32
BF16 = jnp.bfloat16


def exchange_kernel(n, x_hbm, wt_hbm, gt_hbm, xf_hbm, own_hbm, plus_hbm, minus_hbm,
                    xf, wbuf, gbuf, g, part, rbuf, csum, u1buf,
                    x_sem, g_sem, w_sem, ag_send, ag_recv, pr_send, pr_recv,
                    d_send, d_recv, u_send, u_recv, out_sem):
    rows, width = x_hbm.shape
    half = width // 2
    nb = w_sem.shape[0]
    blk = width // nb
    me = lax.axis_index("tp")
    chips = n // 2
    chip, core = me // 2, lax.rem(me, 2)
    c_right, c_left = lax.rem(chip + 1, chips), lax.rem(chip + chips - 1, chips)
    c_opp = lax.rem(chip + 2, chips)
    right, left, opp = 2 * c_right + core, 2 * c_left + core, 2 * c_opp + core
    peer = 2 * chip + 1 - core

    def at(dev, lo=0, size=None):
        r = pl.ds(pl.multiple_of(dev * rows, rows), rows)
        return xf.at[r, pl.ds(lo, width if size is None else size)]

    own_x = pltpu.make_async_copy(x_hbm, at(me), x_sem)
    own_x.start()
    g_load = pltpu.make_async_copy(gt_hbm, gbuf, g_sem)
    g_load.start()
    seq = [j for p in zip(range(nb // 2), range(nb // 2, nb)) for j in p]
    w_loads = {}
    for j in seq:
        cols = pl.ds(j * blk, blk)
        w_loads[j] = pltpu.make_async_copy(wt_hbm.at[:, cols], wbuf.at[:, cols], w_sem.at[j])
        w_loads[j].start()

    barrier = pltpu.get_barrier_semaphore()
    for dev in (peer, left, right):
        pl.semaphore_signal(barrier, inc=1, device_id={"tp": dev}, device_id_type=MESH)
    pl.semaphore_wait(barrier, 3)

    def send(src, dst, s_sem, r_sem, dev):
        cp = pltpu.make_async_remote_copy(src_ref=src, dst_ref=dst, send_sem=s_sem, recv_sem=r_sem,
                                          device_id={"tp": dev}, device_id_type=MESH)
        cp.start()
        return cp

    own_x.wait()
    ag = {}
    ag[0] = send(at(me, 0, half), at(me, 0, half), ag_send.at[0], ag_recv.at[0], right)
    ag[3] = send(at(me, half, half), at(me, half, half), ag_send.at[3], ag_recv.at[3], left)
    ag[1] = send(at(me, half, half), at(me, half, half), ag_send.at[1], ag_recv.at[1], right)
    ag[2] = send(at(me, 0, half), at(me, 0, half), ag_send.at[2], ag_recv.at[2], left)
    pr = {}
    pr[6] = send(at(me), at(me), pr_send.at[6], pr_recv.at[6], peer)

    def arrived(slot, dev, lo):
        pltpu.make_async_remote_copy(src_ref=at(dev, lo, half), dst_ref=at(dev, lo, half), send_sem=ag_send.at[slot],
                                     recv_sem=ag_recv.at[slot], device_id={"tp": me}, device_id_type=MESH).wait_recv()
        pr[slot] = send(at(dev, lo, half), at(dev, lo, half), pr_send.at[slot], pr_recv.at[slot], peer)

    g_load.wait()
    g[...] = gbuf[...].T

    def partial(j):
        w_loads[j].wait()
        cols = pl.ds(j * blk, blk)
        t = jnp.dot(g[...], wbuf[:, cols], preferred_element_type=F32)
        part[:, :, :, cols] = t.reshape(chips, 2, rows, blk)

    d2d = {}

    def to_peer(j):
        cols = pl.ds(j * blk, blk)
        d2d[j] = send(part.at[:, 1 - core, :, cols], rbuf.at[:, :, cols], d_send.at[j], d_recv.at[j], peer)

    u1 = {}

    def chip_sum(j):
        cols = pl.ds(j * blk, blk)
        d2d[j].wait_recv()
        csum[:, :, cols] = part[:, core, :, cols] + rbuf[:, :, cols]
        u1[j] = send(csum.at[c_opp, :, cols], u1buf.at[:, cols], u_send.at[j], u_recv.at[j],
                     right if j < nb // 2 else left)

    partial(seq[0])
    to_peer(seq[0])
    partial(seq[1])
    to_peer(seq[1])
    chip_sum(seq[0])
    partial(seq[2])
    to_peer(seq[2])
    arrived(0, left, 0)
    ag[4] = send(at(left, 0, half), at(left, 0, half), ag_send.at[4], ag_recv.at[4], right)
    arrived(3, right, half)
    ag[5] = send(at(right, half, half), at(right, half, half), ag_send.at[5], ag_recv.at[5], left)
    chip_sum(seq[1])
    partial(seq[3])
    to_peer(seq[3])
    chip_sum(seq[2])
    arrived(1, left, half)
    arrived(2, right, 0)
    chip_sum(seq[3])

    outs = []

    def out(src, dst):
        cp = pltpu.make_async_copy(src, dst, out_sem.at[len(outs)])
        cp.start()
        outs.append(cp)

    lo, hi = pl.ds(0, half), pl.ds(half, half)
    out(csum.at[chip], own_hbm)
    out(csum.at[c_right, :, hi], plus_hbm.at[:, hi])
    out(csum.at[c_left, :, lo], minus_hbm.at[:, lo])

    arrived(4, opp, 0)
    arrived(5, opp, half)
    for cp in pr.values():
        cp.wait()
    out(xf, xf_hbm)

    for j in seq:
        cols = pl.ds(j * blk, blk)
        u1[j].wait_recv()
        c, dst = (c_right, plus_hbm) if j < nb // 2 else (c_left, minus_hbm)
        csum[c, :, cols] += u1buf[:, cols]
        out(csum.at[c, :, cols], dst.at[:, cols])
    for cp in ag.values():
        cp.wait_send()
    for cp in d2d.values():
        cp.wait_send()
    for cp in u1.values():
        cp.wait_send()
    for cp in outs:
        cp.wait()


def exchange(x_blk, wt_blk, gt_blk, n):
    rows, width = x_blk.shape
    cols, tokens = gt_blk.shape
    chips = n // 2
    nb = 4
    hbm = pl.BlockSpec(memory_space=pltpu.HBM)
    part = jax.ShapeDtypeStruct((rows, width), F32)
    return pl.pallas_call(
        functools.partial(exchange_kernel, n),
        out_shape=(jax.ShapeDtypeStruct((tokens, width), BF16), part, part, part),
        in_specs=[hbm] * 3,
        out_specs=(hbm,) * 4,
        scratch_shapes=[
            pltpu.VMEM((tokens, width), BF16),
            pltpu.VMEM((cols, width), BF16),
            pltpu.VMEM((cols, tokens), BF16),
            pltpu.VMEM((tokens, cols), BF16),
            pltpu.VMEM((chips, 2, rows, width), F32),
            pltpu.VMEM((chips, rows, width), F32),
            pltpu.VMEM((chips, rows, width), F32),
            pltpu.VMEM((rows, width), F32),
            pltpu.SemaphoreType.DMA,
            pltpu.SemaphoreType.DMA,
            pltpu.SemaphoreType.DMA((nb,)),
            pltpu.SemaphoreType.DMA((6,)),
            pltpu.SemaphoreType.DMA((6,)),
            pltpu.SemaphoreType.DMA((7,)),
            pltpu.SemaphoreType.DMA((7,)),
            pltpu.SemaphoreType.DMA((nb,)),
            pltpu.SemaphoreType.DMA((nb,)),
            pltpu.SemaphoreType.DMA((nb,)),
            pltpu.SemaphoreType.DMA((nb,)),
            pltpu.SemaphoreType.DMA((4 + nb,)),
        ],
        compiler_params=pltpu.CompilerParams(collective_id=0, has_side_effects=True, vmem_limit_bytes=60 * 2**20),
        cost_estimate=pl.CostEstimate(flops=2 * tokens * width * cols, bytes_accessed=2 * width * cols,
                                      transcendentals=0),
        name="exchange",
    )(x_blk, wt_blk, gt_blk)


def weight_kernel(x_hbm, gt_hbm, o_hbm, xbuf, gbuf, obuf, x_sem, g_sem, o_sem):
    cols = gbuf.shape[0]
    blk = 256
    starts = [0] + list(range(cols % blk, cols, blk)) if cols % blk else list(range(0, cols, blk))
    ends = starts[1:] + [cols]
    x_load = pltpu.make_async_copy(x_hbm, xbuf, x_sem)
    x_load.start()
    g_load = pltpu.make_async_copy(gt_hbm, gbuf, g_sem)
    g_load.start()
    g_load.wait()
    x_load.wait()
    stores = []
    for i, (a, b) in enumerate(zip(starts, ends)):
        r = pl.ds(a, b - a)
        obuf[r, :] = jnp.dot(gbuf[r, :], xbuf[...], preferred_element_type=F32)
        cp = pltpu.make_async_copy(obuf.at[r, :], o_hbm.at[r, :], o_sem.at[i])
        cp.start()
        stores.append(cp)
    for cp in stores:
        cp.wait()


def weight_grad(x_full, gt_blk):
    tokens, width = x_full.shape
    cols = gt_blk.shape[0]
    hbm = pl.BlockSpec(memory_space=pltpu.HBM)
    return pl.pallas_call(
        weight_kernel,
        out_shape=jax.ShapeDtypeStruct((cols, width), F32),
        in_specs=[hbm] * 2,
        out_specs=hbm,
        scratch_shapes=[
            pltpu.VMEM((tokens, width), BF16),
            pltpu.VMEM((cols, tokens), BF16),
            pltpu.VMEM((cols, width), F32),
            pltpu.SemaphoreType.DMA,
            pltpu.SemaphoreType.DMA,
            pltpu.SemaphoreType.DMA((16,)),
        ],
        compiler_params=pltpu.CompilerParams(vmem_limit_bytes=60 * 2**20),
        cost_estimate=pl.CostEstimate(flops=2 * tokens * width * cols, bytes_accessed=4 * width * cols,
                                      transcendentals=0),
        name="weight_grad",
    )(x_full, gt_blk)


def solution(mesh):
    n = mesh.shape["tp"]

    def per_device(x_blk, w_blk, grad_blk):
        gt_blk = grad_blk.T
        x_full, own, plus, minus = exchange(x_blk, w_blk.T, gt_blk, n)
        from_left = lax.ppermute(plus, "tp", [(i, (i + 2) % n) for i in range(n)])
        from_right = lax.ppermute(minus, "tp", [(i, (i + n - 2) % n) for i in range(n)])
        grad_w = weight_grad(x_full, gt_blk).T
        grad_x = (own + from_left + from_right).astype(BF16)
        return grad_x, grad_w

    return jax.shard_map(
        per_device,
        mesh=mesh,
        in_specs=(P(("dp", "tp"), None), P(None, "tp"), P("dp", "tp")),
        out_specs=(P(("dp", "tp"), None), P("dp", "tp")),
        check_vma=False,
    )
```

time: 77.4 us -> 41.9 us (0.54)
  Pallas kernels: 0 us -> 37.1 us
  waiting for transfers between devices: 34.8 us -> 0.01 us
  matrix products: 26 us -> 0 us
  between operations: 14.1 us -> 0.67 us
  starting transfers between devices: 0.12 us -> 3.31 us
  other arithmetic: 1.73 us -> 0.76 us
    pallas_call x0 -> x2, Pallas kernels: none -> 37.1 us  [the longest x1 23.3 us: exchange(): pl.pallas_call(functools.partial(exchange_kernel, n), out_shape=(jax.Shap...]
    dot_general x2 -> x0, matrix products: 26 us -> none  [the longest x1 15.7 us: per_device(): lax.dot_general(x_full, grad_blk, (((0,), (0,)), ((), ())), preferred_ele...]
    reduce_scatter x1 -> x0, waiting for transfers between devices: 19.8 us -> none  [per_device(): lax.psum_scatter(part_dx, 'tp', scatter_dimension=0, tiled=True)]
    all_gather x1 -> x0, waiting for transfers between devices: 14.2 us -> none  [per_device(): x_full = lax.all_gather(x_blk, 'tp', axis=0, tiled=True)]
    ppermute x0 -> x2, starting transfers between devices: none -> 3.31 us  [the longest x1 2.8 us: per_device(): lax.ppermute(minus, 'tp', [(i, (i + n - 2) % n) for i in range(n)])]
    convert_element_type x1, other arithmetic: 1.73 us -> 0.76 us  [per_device(): grad_x = (own + from_left + from_right).astype(BF16)]
  transfers between devices with their start and end apart: 2 -> 2, of which waited for: 2 -> 0; matrix products, arithmetic and copies ran while one was open for 34% -> 0% of each run, Pallas kernels for 0% -> 33%
where the time goes in v1:
time: 41.9 us; the launch traced here: 41.8 us
  Pallas kernels  37.1 us (89%)
  starting transfers between devices  3.31 us (8%)
  other arithmetic  0.76 us (2%)
  between operations  0.67 us (2%)
    pallas_call x1, Pallas kernels, exchange(): pl.pallas_call(functools.partial(exchange_kernel, n), out_shape=(jax.Shap...  23.3 us
    pallas_call x1, Pallas kernels, weight_grad(): pl.pallas_call(weight_kernel, out_shape=jax.ShapeDtypeStruct((cols, width...  13.8 us
    ppermute x1, starting transfers between devices, per_device(): lax.ppermute(minus, 'tp', [(i, (i + n - 2) % n) for i in range(n)])  2.8 us
  transfers between devices with their start and end apart: 2, of which 0 were waited for; matrix products, arithmetic and copies ran while one was open for 0% of the time, Pallas kernels for 33%

profile of v1, /device:TPU:112, one launch (start us, length us, event | category | flops | bytes accessed | tf_op | source)
XLA Modules:
  0.0 41.8 jit_solution(10459794689510849764)
XLA Ops:
  0.6 23.3 %exchange.1 = (bf16[256,3584]{1,0:T(8,128)(2,1)}, f32[32,3584]{1,0:T(8,128)}, f32[32,3584]{1,0:T(8,128)}, f32[32,3584]{1,0:T(8,128)}) custom-call(bf16[32,3584]{1,0:T(8,128)(2,1)} %x_hbm.1, bf16[2368,3584]{1,0:T(8,128)(2,1)} %bitcast.4, bf16[2368,256]{1,0:T(8,128)(2,1)} %bitcast.5), custom_call_target="tpu_custom_call" | custom-call | flops 4345298944 | bytes 16973824 | tf_op jit(solution)/shard_map/exchange/pallas_call | solution.py:155
  24.0 0.5 %collective-permute-start = (f32[32,3584]{1,0:T(8,128)}, f32[32,3584]{1,0:T(8,128)S(1)}, u32[]{:S(2)}, u32[]{:S(2)}) collective-permute-start(f32[32,3584]{1,0:T(8,128)} %get-tuple-element.7), channel_id=1, source_target_pairs={{0,2},{1,3},{2,4},{3,5},{4,6},{5,7},{6,0},{7,1},{8,10},{9,11},{10,... | collective-permute-start | bytes 1376264 | tf_op jit(solution)/shard_map/ppermute | solution.py:241
  24.5 2.8 %collective-permute-start.1 = (f32[32,3584]{1,0:T(8,128)}, f32[32,3584]{1,0:T(8,128)S(1)}, u32[]{:S(2)}, u32[]{:S(2)}) collective-permute-start(f32[32,3584]{1,0:T(8,128)} %get-tuple-element.8), channel_id=1, source_target_pairs={{0,6},{1,7},{2,0},{3,1},{4,2},{5,3},{6,4},{7,5},{8,14},{9,15},{10,... | collective-permute-start | bytes 1376264 | tf_op jit(solution)/shard_map/ppermute | solution.py:242
  27.3 0.0 copy-start
  27.3 13.8 %weight_grad.1 = f32[2368,3584]{1,0:T(8,128)} custom-call(bf16[256,3584]{1,0:T(8,128)(2,1)} %get-tuple-element.9.x_hbm, bf16[2368,256]{1,0:T(8,128)(2,1)} %bitcast.6), custom_call_target="tpu_custom_call" | custom-call | flops 4345298944 | bytes 33947648 | tf_op jit(solution)/shard_map/weight_grad/pallas_call | solution.py:215
  41.1 0.0 collective-permute-done
  41.1 0.0 collective-permute-done.1
  41.1 0.0 copy-done
  41.1 0.8 %add_convert_fusion = bf16[32,3584]{1,0:T(8,128)(2,1)} fusion(f32[32,3584]{1,0:T(8,128)S(1)} %collective-permute-done.1, f32[32,3584]{1,0:T(8,128)S(1)} %copy-done, f32[32,3584]{1,0:T(8,128)S(1)} %collective-permute-done), kind=kLoop, calls=%fused_computation | loop fusion | flops 344064 | bytes 1605632 | tf_op jit(solution)/shard_map/convert_element_type | solution.py:244
Async XLA Ops:
  24.0 17.1 %collective-permute-start = (f32[32,3584]{1,0:T(8,128)}, f32[32,3584]{1,0:T(8,128)S(1)}, u32[]{:S(2)}, u32[]{:S(2)}) collective-permute-start(f32[32,3584]{1,0:T(8,128)} %get-tuple-element.7), channel_id=1, source_target_pairs={{0,2},{1,3},{2,4},{3,5},{4,6},{5,7},{6,0},{7,1},{8,10},{9,11},{10,... | collective-permute-start | bytes 1376264 | tf_op jit(solution)/shard_map/ppermute | solution.py:241
  24.5 16.6 %collective-permute-start.1 = (f32[32,3584]{1,0:T(8,128)}, f32[32,3584]{1,0:T(8,128)S(1)}, u32[]{:S(2)}, u32[]{:S(2)}) collective-permute-start(f32[32,3584]{1,0:T(8,128)} %get-tuple-element.8), channel_id=1, source_target_pairs={{0,6},{1,7},{2,0},{3,1},{4,2},{5,3},{6,4},{7,5},{8,14},{9,15},{10,... | collective-permute-start | bytes 1376264 | tf_op jit(solution)/shard_map/ppermute | solution.py:242
  27.3 13.8 %copy-start = (f32[32,3584]{1,0:T(8,128)S(1)}, f32[32,3584]{1,0:T(8,128)}, u32[]{:S(2)}) copy-start(f32[32,3584]{1,0:T(8,128)} %get-tuple-element.6) | copy-start | bytes 1376260

commit v2 on v0

v2 whole, which is shorter than its diff:
```python
import functools

import jax
import jax.numpy as jnp
from jax import lax
from jax.experimental import pallas as pl
from jax.experimental.pallas import tpu as pltpu
from jax.sharding import PartitionSpec as P

MESH = pl.DeviceIdType.MESH
F32 = jnp.float32
BF16 = jnp.bfloat16


def exchange_kernel(n, groups, x_hbm, wt_hbm, gt_hbm, xf, gt, own, plus, minus,
                    wbuf, g, part, rbuf, opp_sum, u1buf,
                    x_sem, g_sem, w_sem, ag_send, ag_recv, pr_send, pr_recv,
                    d_send, d_recv, u_send, u_recv):
    rows, width = x_hbm.shape
    half = rows // 2
    nb = w_sem.shape[0]
    blk = width // nb
    me = lax.axis_index("tp")
    chips = n // 2
    chip, core = me // 2, lax.rem(me, 2)
    c_right, c_left = lax.rem(chip + 1, chips), lax.rem(chip + chips - 1, chips)
    c_opp = lax.rem(chip + 2, chips)
    right, left, opp = 2 * c_right + core, 2 * c_left + core, 2 * c_opp + core
    peer = 2 * chip + 1 - core
    lo, hi = pl.ds(0, half), pl.ds(half, half)

    def at(dev, part_of=0, size=rows):
        return xf.at[pl.ds(pl.multiple_of(dev * rows + part_of * half, half), size), :]

    def low(dev):
        return at(dev, 0, half)

    def high(dev):
        return at(dev, 1, half)

    own_x = pltpu.make_async_copy(x_hbm, at(me), x_sem)
    own_x.start()
    g_load = pltpu.make_async_copy(gt_hbm, gt, g_sem)
    g_load.start()
    ahead = 3

    def w_load(j):
        cols = pl.ds(j * blk, blk)
        return pltpu.make_async_copy(wt_hbm.at[:, cols], wbuf.at[:, cols], w_sem.at[j])

    for j in range(ahead):
        w_load(j).start()

    barrier = pltpu.get_barrier_semaphore()
    for dev in (left, right, peer):
        pl.semaphore_signal(barrier, inc=1, device_id={"tp": dev}, device_id_type=MESH)
    pl.semaphore_wait(barrier, 3)

    def send(src, dst, s_sem, r_sem, dev):
        cp = pltpu.make_async_remote_copy(src_ref=src, dst_ref=dst, send_sem=s_sem, recv_sem=r_sem,
                                          device_id={"tp": dev}, device_id_type=MESH)
        cp.start()
        return cp

    own_x.wait()
    ag = {}
    ag[0] = send(low(me), low(me), ag_send.at[0], ag_recv.at[0], right)
    ag[3] = send(high(me), high(me), ag_send.at[3], ag_recv.at[3], left)
    ag[1] = send(high(me), high(me), ag_send.at[1], ag_recv.at[1], right)
    ag[2] = send(low(me), low(me), ag_send.at[2], ag_recv.at[2], left)
    pr = {}
    pr[6] = send(at(me), at(me), pr_send.at[6], pr_recv.at[6], peer)

    def arrived(slot, block, onward=None):
        pltpu.make_async_remote_copy(src_ref=block, dst_ref=block, send_sem=ag_send.at[slot],
                                     recv_sem=ag_recv.at[slot], device_id={"tp": me}, device_id_type=MESH).wait_recv()
        if onward is not None:
            to, dev = onward
            ag[to] = send(block, block, ag_send.at[to], ag_recv.at[to], dev)
        pr[slot] = send(block, block, pr_send.at[slot], pr_recv.at[slot], peer)

    g_load.wait()
    g[...] = gt[...].T

    d2d = {}

    def partial(j):
        w_load(j).wait()
        if j + ahead < nb:
            w_load(j + ahead).start()
        cols = pl.ds(j * blk, blk)
        t = jnp.dot(g[...], wbuf[:, cols], preferred_element_type=F32)
        part[:, :, :, cols] = t.reshape(chips, 2, rows, blk)
        d2d[j] = send(part.at[:, 1 - core, :, cols], rbuf.at[:, :, cols], d_send.at[j], d_recv.at[j], peer)

    u1 = []

    def chip_sum(js):
        for j in js:
            cols = pl.ds(j * blk, blk)
            d2d[j].wait_recv()
            opp_sum[:, cols] = part[c_opp, core, :, cols] + rbuf[c_opp, :, cols]
            own[:, cols] = part[chip, core, :, cols] + rbuf[chip, :, cols]
            plus[:, cols] = part[c_right, core, :, cols] + rbuf[c_right, :, cols]
            minus[:, cols] = part[c_left, core, :, cols] + rbuf[c_left, :, cols]
        cols = pl.ds(js[0] * blk, len(js) * blk)
        k = len(u1)
        u1.append((js, send(opp_sum.at[lo, cols], u1buf.at[lo, cols], u_send.at[0, k], u_recv.at[0, k], right),
                   send(opp_sum.at[hi, cols], u1buf.at[hi, cols], u_send.at[1, k], u_recv.at[1, k], left)))

    for j in range(4):
        partial(j)
    arrived(0, low(left), (4, right))
    arrived(3, high(right), (5, left))
    chip_sum(groups[0])
    partial(4)
    arrived(1, high(left))
    arrived(2, low(right))
    partial(5)
    partial(6)
    chip_sum(groups[1])
    chip_sum(groups[2])
    arrived(4, low(opp))
    arrived(5, high(opp))
    for js, from_left, from_right in u1:
        cols = pl.ds(js[0] * blk, len(js) * blk)
        from_left.wait_recv()
        plus[lo, cols] += u1buf[lo, cols]
        from_right.wait_recv()
        minus[hi, cols] += u1buf[hi, cols]
    for cp in pr.values():
        cp.wait()
    for cp in ag.values():
        cp.wait_send()
    for cp in d2d.values():
        cp.wait_send()
    for _, a, b in u1:
        a.wait_send()
        b.wait_send()


def exchange(x_blk, wt_blk, gt_blk, n):
    rows, width = x_blk.shape
    cols, tokens = gt_blk.shape
    chips = n // 2
    nb = 7
    groups = ((0, 1, 2, 3), (4, 5), (6,))
    hbm = pl.BlockSpec(memory_space=pltpu.HBM)
    vmem = pl.BlockSpec(memory_space=pltpu.VMEM)
    part = pltpu.VMEM((rows, width), F32)
    return pl.pallas_call(
        functools.partial(exchange_kernel, n, groups),
        out_shape=(pltpu.VMEM((tokens, width), BF16), pltpu.VMEM((cols, tokens), BF16), part, part, part),
        in_specs=[hbm] * 3,
        out_specs=(vmem,) * 5,
        scratch_shapes=[
            pltpu.VMEM((cols, width), BF16),
            pltpu.VMEM((tokens, cols), BF16),
            pltpu.VMEM((chips, 2, rows, width), F32),
            pltpu.VMEM((chips, rows, width), F32),
            pltpu.VMEM((rows, width), F32),
            pltpu.VMEM((rows, width), F32),
            pltpu.SemaphoreType.DMA,
            pltpu.SemaphoreType.DMA,
            pltpu.SemaphoreType.DMA((nb,)),
            pltpu.SemaphoreType.DMA((6,)),
            pltpu.SemaphoreType.DMA((6,)),
            pltpu.SemaphoreType.DMA((7,)),
            pltpu.SemaphoreType.DMA((7,)),
            pltpu.SemaphoreType.DMA((nb,)),
            pltpu.SemaphoreType.DMA((nb,)),
            pltpu.SemaphoreType.DMA((2, len(groups))),
            pltpu.SemaphoreType.DMA((2, len(groups))),
        ],
        compiler_params=pltpu.CompilerParams(collective_id=0, has_side_effects=True, vmem_limit_bytes=32 * 2**20),
        cost_estimate=pl.CostEstimate(flops=2 * tokens * width * cols, bytes_accessed=2 * width * cols,
                                      transcendentals=0),
        name="exchange",
    )(*(pltpu.with_memory_space_constraint(a, pltpu.HBM) for a in (x_blk, wt_blk, gt_blk)))


def weight_kernel(x, gt, o_hbm, obuf, o_sem):
    cols = gt.shape[0]
    blk = 256
    starts = ([0] if cols % blk else []) + list(range(cols % blk, cols, blk))
    ends = starts[1:] + [cols]
    stores = []
    for i, (a, b) in enumerate(zip(starts, ends)):
        r = pl.ds(a, b - a)
        obuf[r, :] = jnp.dot(gt[r, :], x[...], preferred_element_type=F32)
        cp = pltpu.make_async_copy(obuf.at[r, :], o_hbm.at[r, :], o_sem.at[i])
        cp.start()
        stores.append(cp)
    for cp in stores:
        cp.wait()


def weight_grad(x_full, gt_blk):
    tokens, width = x_full.shape
    cols = gt_blk.shape[0]
    vmem = pl.BlockSpec(memory_space=pltpu.VMEM)
    return pl.pallas_call(
        weight_kernel,
        out_shape=jax.ShapeDtypeStruct((cols, width), F32),
        in_specs=[vmem] * 2,
        out_specs=pl.BlockSpec(memory_space=pltpu.HBM),
        scratch_shapes=[pltpu.VMEM((cols, width), F32), pltpu.SemaphoreType.DMA((16,))],
        compiler_params=pltpu.CompilerParams(vmem_limit_bytes=40 * 2**20),
        cost_estimate=pl.CostEstimate(flops=2 * tokens * width * cols, bytes_accessed=4 * width * cols,
                                      transcendentals=0),
        name="weight_grad",
    )(x_full, gt_blk)


def solution(mesh):
    n = mesh.shape["tp"]

    def per_device(x_blk, w_blk, grad_blk):
        x_full, gt_blk, own, plus, minus = exchange(x_blk, w_blk.T, grad_blk.T, n)
        from_left = lax.ppermute(plus, "tp", [(i, (i + 2) % n) for i in range(n)])
        from_right = lax.ppermute(minus, "tp", [(i, (i + n - 2) % n) for i in range(n)])
        grad_w = weight_grad(x_full, gt_blk).T
        grad_x = (own + from_left + from_right).astype(BF16)
        return grad_x, grad_w

    return jax.shard_map(
        per_device,
        mesh=mesh,
        in_specs=(P(("dp", "tp"), None), P(None, "tp"), P("dp", "tp")),
        out_specs=(P(("dp", "tp"), None), P("dp", "tp")),
        check_vma=False,
    )
```

time: 77.4 us -> 37 us (0.48)
  waiting for transfers between devices: 34.8 us -> 0.01 us
  Pallas kernels: 0 us -> 32.2 us
  matrix products: 26 us -> 0 us
  between operations: 14.1 us -> 0.66 us
  starting transfers between devices: 0.12 us -> 3.31 us
  other arithmetic: 1.73 us -> 0.76 us
    pallas_call x0 -> x2, Pallas kernels: none -> 32.2 us  [the longest x1 20.3 us: exchange(): pl.pallas_call(functools.partial(exchange_kernel, n, groups), out_shape=(...]
    dot_general x2 -> x0, matrix products: 26 us -> none  [the longest x1 15.7 us: per_device(): lax.dot_general(x_full, grad_blk, (((0,), (0,)), ((), ())), preferred_ele...]
    reduce_scatter x1 -> x0, waiting for transfers between devices: 19.8 us -> none  [per_device(): lax.psum_scatter(part_dx, 'tp', scatter_dimension=0, tiled=True)]
    all_gather x1 -> x0, waiting for transfers between devices: 14.2 us -> none  [per_device(): x_full = lax.all_gather(x_blk, 'tp', axis=0, tiled=True)]
    ppermute x0 -> x2, starting transfers between devices: none -> 3.31 us  [the longest x1 2.42 us: per_device(): lax.ppermute(minus, 'tp', [(i, (i + n - 2) % n) for i in range(n)])]
    convert_element_type x1, other arithmetic: 1.73 us -> 0.76 us  [per_device(): grad_x = (own + from_left + from_right).astype(BF16)]
  transfers between devices with their start and end apart: 2 -> 2, of which waited for: 2 -> 0; matrix products, arithmetic and copies ran while one was open for 34% -> 0% of each run, Pallas kernels for 0% -> 32%
where the time goes in v2:
time: 37 us; the launch traced here: 36.9 us
  Pallas kernels  32.2 us (87%)
  starting transfers between devices  3.31 us (9%)
  other arithmetic  0.76 us (2%)
  between operations  0.66 us (2%)
    pallas_call x1, Pallas kernels, exchange(): pl.pallas_call(functools.partial(exchange_kernel, n, groups), out_shape=(...  20.3 us
    pallas_call x1, Pallas kernels, weight_grad(): pl.pallas_call(weight_kernel, out_shape=jax.ShapeDtypeStruct((cols, width...  11.9 us
    ppermute x1, starting transfers between devices, per_device(): lax.ppermute(minus, 'tp', [(i, (i + n - 2) % n) for i in range(n)])  2.42 us
    ppermute x1, starting transfers between devices, per_device(): from_left = lax.ppermute(plus, 'tp', [(i, (i + 2) % n) for i in range(n)])  0.89 us
    convert_element_type x1, other arithmetic, per_device(): grad_x = (own + from_left + from_right).astype(BF16)  0.76 us
  transfers between devices with their start and end apart: 2, of which 0 were waited for; matrix products, arithmetic and copies ran while one was open for 0% of the time, Pallas kernels for 32%

profile of v2, /device:TPU:112, one launch (start us, length us, event | category | flops | bytes accessed | tf_op | source)
XLA Modules:
  0.0 36.9 jit_solution(454954207197645659)
XLA Ops:
  0.6 20.3 %exchange.1 = (bf16[256,3584]{1,0:T(8,128)(2,1)S(1)}, bf16[2368,256]{1,0:T(8,128)(2,1)S(1)}, f32[32,3584]{1,0:T(8,128)S(1)}, f32[32,3584]{1,0:T(8,128)S(1)}, f32[32,3584]{1,0:T(8,128)S(1)}) custom-call(bf16[32,3584]{1,0:T(8,128)(2,1)} %x_hbm.1, bf16[2368,3584]{1,0:T(8,128)(2,1)} %bitcast.4, bf16[2368,256]{1,0:T(8,128)(2,1)} %bitcast.5), custom_call_target="tpu_custom_call" | custom-call | flops 4345298944 | bytes 16973824 | tf_op jit(solution)/shard_map/exchange/pallas_call | solution.py:151
  21.0 0.9 %collective-permute-start = (f32[32,3584]{1,0:T(8,128)S(1)}, f32[32,3584]{1,0:T(8,128)S(1)}, u32[]{:S(2)}, u32[]{:S(2)}) collective-permute-start(f32[32,3584]{1,0:T(8,128)S(1)} %get-tuple-element.8), channel_id=1, source_target_pairs={{0,2},{1,3},{2,4},{3,5},{4,6},{5,7},{6,0},{7,1},{8,10},{9,11},{10,... | collective-permute-start | bytes 1376264 | tf_op jit(solution)/shard_map/ppermute | solution.py:220
  21.8 2.4 %collective-permute-start.1 = (f32[32,3584]{1,0:T(8,128)S(1)}, f32[32,3584]{1,0:T(8,128)S(1)}, u32[]{:S(2)}, u32[]{:S(2)}) collective-permute-start(f32[32,3584]{1,0:T(8,128)S(1)} %get-tuple-element.9), channel_id=1, source_target_pairs={{0,6},{1,7},{2,0},{3,1},{4,2},{5,3},{6,4},{7,5},{8,14},{9,15},{10,... | collective-permute-start | bytes 1376264 | tf_op jit(solution)/shard_map/ppermute | solution.py:221
  24.3 11.9 %weight_grad.1 = f32[2368,3584]{1,0:T(8,128)} custom-call(bf16[256,3584]{1,0:T(8,128)(2,1)S(1)} %get-tuple-element.10.x, bf16[2368,256]{1,0:T(8,128)(2,1)S(1)} %get-tuple-element.11.gt), custom_call_target="tpu_custom_call" | custom-call | flops 4345298944 | bytes 33947648 | tf_op jit(solution)/shard_map/weight_grad/pallas_call | solution.py:202
  36.1 0.0 collective-permute-done
  36.2 0.0 collective-permute-done.1
  36.2 0.8 %add_convert_fusion = bf16[32,3584]{1,0:T(8,128)(2,1)} fusion(f32[32,3584]{1,0:T(8,128)S(1)} %collective-permute-done.1, f32[32,3584]{1,0:T(8,128)S(1)} %get-tuple-element.7, f32[32,3584]{1,0:T(8,128)S(1)} %collective-permute-done), kind=kLoop, calls=%fused_computation | loop fusion | flops 344064 | bytes 1605632 | tf_op jit(solution)/shard_map/convert_element_type | solution.py:223
Async XLA Ops:
  21.0 15.2 %collective-permute-start = (f32[32,3584]{1,0:T(8,128)S(1)}, f32[32,3584]{1,0:T(8,128)S(1)}, u32[]{:S(2)}, u32[]{:S(2)}) collective-permute-start(f32[32,3584]{1,0:T(8,128)S(1)} %get-tuple-element.8), channel_id=1, source_target_pairs={{0,2},{1,3},{2,4},{3,5},{4,6},{5,7},{6,0},{7,1},{8,10},{9,11},{10,... | collective-permute-start | bytes 1376264 | tf_op jit(solution)/shard_map/ppermute | solution.py:220
  21.8 14.3 %collective-permute-start.1 = (f32[32,3584]{1,0:T(8,128)S(1)}, f32[32,3584]{1,0:T(8,128)S(1)}, u32[]{:S(2)}, u32[]{:S(2)}) collective-permute-start(f32[32,3584]{1,0:T(8,128)S(1)} %get-tuple-element.9), channel_id=1, source_target_pairs={{0,6},{1,7},{2,0},{3,1},{4,2},{5,3},{6,4},{7,5},{8,14},{9,15},{10,... | collective-permute-start | bytes 1376264 | tf_op jit(solution)/shard_map/ppermute | solution.py:221

commit v3 on v2

v3 whole, which is shorter than its diff:
```python
import functools

import jax
import jax.numpy as jnp
from jax import lax
from jax.experimental import pallas as pl
from jax.experimental.pallas import tpu as pltpu
from jax.sharding import PartitionSpec as P

MESH = pl.DeviceIdType.MESH
F32 = jnp.float32
BF16 = jnp.bfloat16


def exchange_kernel(n, x_hbm, wt_hbm, gt_hbm, xf, gt, own, plus, minus,
                    wbuf, g, part, rbuf, opp_sum, u1buf,
                    x_sem, g_sem, w_sem, ag_send, ag_recv, pr_send, pr_recv,
                    d_send, d_recv, u_send, u_recv):
    rows, width = x_hbm.shape
    half = rows // 2
    nb = w_sem.shape[0]
    blk = width // nb
    me = lax.axis_index("tp")
    chips = n // 2
    chip, core = me // 2, lax.rem(me, 2)
    c_right, c_left = lax.rem(chip + 1, chips), lax.rem(chip + chips - 1, chips)
    c_opp = lax.rem(chip + 2, chips)
    right, left, opp = 2 * c_right + core, 2 * c_left + core, 2 * c_opp + core
    peer = 2 * chip + 1 - core
    lo, hi = pl.ds(0, half), pl.ds(half, half)

    def at(dev, part_of=0, size=rows):
        return xf.at[pl.ds(pl.multiple_of(dev * rows + part_of * half, half), size), :]

    def low(dev):
        return at(dev, 0, half)

    def high(dev):
        return at(dev, 1, half)

    own_x = pltpu.make_async_copy(x_hbm, at(me), x_sem)
    own_x.start()
    g_load = pltpu.make_async_copy(gt_hbm, gt, g_sem)
    g_load.start()
    ahead = 4

    def w_load(j):
        cols = pl.ds(pl.multiple_of(j * blk, blk), blk)
        return pltpu.make_async_copy(wt_hbm.at[:, cols], wbuf.at[:, cols], w_sem.at[j])

    for j in range(ahead):
        w_load(j).start()

    barrier = pltpu.get_barrier_semaphore()
    for dev in (left, right, peer):
        pl.semaphore_signal(barrier, inc=1, device_id={"tp": dev}, device_id_type=MESH)
    pl.semaphore_wait(barrier, 3)

    def remote(src, dst, s_sem, r_sem, dev):
        return pltpu.make_async_remote_copy(src_ref=src, dst_ref=dst, send_sem=s_sem, recv_sem=r_sem,
                                            device_id={"tp": dev}, device_id_type=MESH)

    def gather(slot, src, dev):
        remote(src, src, ag_send.at[slot], ag_recv.at[slot], dev).start()

    def relay(slot, src):
        return remote(src, src, pr_send.at[slot], pr_recv.at[slot], peer)

    own_x.wait()
    gather(0, low(me), right)
    gather(3, high(me), left)
    gather(1, high(me), right)
    gather(2, low(me), left)
    relay(6, at(me)).start()

    def arrived(slot, src, onward=None):
        remote(src, src, ag_send.at[slot], ag_recv.at[slot], me).wait_recv()
        if onward is not None:
            gather(onward[0], src, onward[1])
        relay(slot, src).start()

    g_load.wait()
    g[...] = gt[...].T

    def block(j):
        return pl.ds(pl.multiple_of(j * blk, blk), blk)

    def to_peer(j):
        return pltpu.make_async_remote_copy(
            src_ref=part.at[:, 1 - core, :, block(j)], dst_ref=rbuf.at[:, :, block(j)],
            send_sem=d_send.at[j], recv_sem=d_recv.at[j], device_id={"tp": peer}, device_id_type=MESH)

    def onward(j, side, dev):
        src = opp_sum.at[side, block(j)]
        k = 0 if side is lo else 1
        return pltpu.make_async_remote_copy(
            src_ref=src, dst_ref=u1buf.at[side, block(j)], send_sem=u_send.at[k, j], recv_sem=u_recv.at[k, j],
            device_id={"tp": dev}, device_id_type=MESH)

    def chip_sum(j):
        to_peer(j).wait_recv()
        cols = block(j)
        opp_sum[:, cols] = part[c_opp, core, :, cols] + rbuf[c_opp, :, cols]
        own[:, cols] = part[chip, core, :, cols] + rbuf[chip, :, cols]
        plus[:, cols] = part[c_right, core, :, cols] + rbuf[c_right, :, cols]
        minus[:, cols] = part[c_left, core, :, cols] + rbuf[c_left, :, cols]
        onward(j, lo, right).start()
        onward(j, hi, left).start()

    lag = 3

    def step(j, carry):
        w_load(j).wait()

        @pl.when(j + ahead < nb)
        def _():
            w_load(j + ahead).start()

        t = jnp.dot(g[...], wbuf[:, block(j)], preferred_element_type=F32)
        part[:, :, :, block(j)] = t.reshape(chips, 2, rows, blk)
        to_peer(j).start()

        @pl.when(j == lag)
        def _():
            arrived(0, low(left), (4, right))
            arrived(3, high(right), (5, left))

        @pl.when(j == lag + 1)
        def _():
            arrived(1, high(left))
            arrived(2, low(right))

        @pl.when(j >= lag)
        def _():
            chip_sum(j - lag)

        return carry

    def each(first, last, f):
        def body(j, carry):
            f(j)
            return carry

        lax.fori_loop(first, last, body, 0)

    lax.fori_loop(0, nb, step, 0)
    each(nb - lag, nb, chip_sum)
    arrived(4, low(opp))
    arrived(5, high(opp))

    def finish(j):
        onward(j, lo, right).wait_recv()
        plus[lo, block(j)] += u1buf[lo, block(j)]
        onward(j, hi, left).wait_recv()
        minus[hi, block(j)] += u1buf[hi, block(j)]

    each(0, nb, finish)
    for slot, block_x in ((0, low(left)), (1, high(left)), (2, low(right)), (3, high(right)), (4, low(opp)),
                          (5, high(opp)), (6, at(me))):
        relay(slot, block_x).wait()
        if slot < 6:
            remote(block_x, block_x, ag_send.at[slot], ag_recv.at[slot], me).wait_send()

    def drain(j):
        to_peer(j).wait_send()
        onward(j, lo, right).wait_send()
        onward(j, hi, left).wait_send()

    each(0, nb, drain)


def exchange(x_blk, wt_blk, gt_blk, n):
    rows, width = x_blk.shape
    cols, tokens = gt_blk.shape
    chips = n // 2
    nb = 7
    hbm = pl.BlockSpec(memory_space=pltpu.HBM)
    vmem = pl.BlockSpec(memory_space=pltpu.VMEM)
    part = pltpu.VMEM((rows, width), F32)
    return pl.pallas_call(
        functools.partial(exchange_kernel, n),
        out_shape=(pltpu.VMEM((tokens, width), BF16), pltpu.VMEM((cols, tokens), BF16), part, part, part),
        in_specs=[hbm] * 3,
        out_specs=(vmem,) * 5,
        scratch_shapes=[
            pltpu.VMEM((cols, width), BF16),
            pltpu.VMEM((tokens, cols), BF16),
            pltpu.VMEM((chips, 2, rows, width), F32),
            pltpu.VMEM((chips, rows, width), F32),
            pltpu.VMEM((rows, width), F32),
            pltpu.VMEM((rows, width), F32),
            pltpu.SemaphoreType.DMA,
            pltpu.SemaphoreType.DMA,
            pltpu.SemaphoreType.DMA((nb,)),
            pltpu.SemaphoreType.DMA((6,)),
            pltpu.SemaphoreType.DMA((6,)),
            pltpu.SemaphoreType.DMA((7,)),
            pltpu.SemaphoreType.DMA((7,)),
            pltpu.SemaphoreType.DMA((nb,)),
            pltpu.SemaphoreType.DMA((nb,)),
            pltpu.SemaphoreType.DMA((2, nb)),
            pltpu.SemaphoreType.DMA((2, nb)),
        ],
        compiler_params=pltpu.CompilerParams(collective_id=0, has_side_effects=True, vmem_limit_bytes=32 * 2**20),
        cost_estimate=pl.CostEstimate(flops=2 * tokens * width * cols, bytes_accessed=2 * width * cols,
                                      transcendentals=0),
        name="exchange",
    )(*(pltpu.with_memory_space_constraint(a, pltpu.HBM) for a in (x_blk, wt_blk, gt_blk)))


def weight_kernel(x, gt, o_hbm, obuf, o_sem):
    cols = gt.shape[0]
    blk = 256
    rest = cols % blk

    def store(start, size, sem):
        return pltpu.make_async_copy(obuf.at[pl.ds(start, size), :], o_hbm.at[pl.ds(start, size), :], sem)

    def rows_of(start, size, sem):
        obuf[pl.ds(start, size), :] = jnp.dot(gt[pl.ds(start, size), :], x[...], preferred_element_type=F32)
        store(start, size, sem).start()

    def at(i):
        return pl.multiple_of(rest + i * blk, 64)

    if rest:
        rows_of(0, rest, o_sem.at[cols // blk])

    def step(i, carry):
        rows_of(at(i), blk, o_sem.at[i])
        return carry

    def drain(i, carry):
        store(at(i), blk, o_sem.at[i]).wait()
        return carry

    lax.fori_loop(0, cols // blk, step, 0)
    lax.fori_loop(0, cols // blk, drain, 0)
    if rest:
        store(0, rest, o_sem.at[cols // blk]).wait()


def weight_grad(x_full, gt_blk):
    tokens, width = x_full.shape
    cols = gt_blk.shape[0]
    vmem = pl.BlockSpec(memory_space=pltpu.VMEM)
    return pl.pallas_call(
        weight_kernel,
        out_shape=jax.ShapeDtypeStruct((cols, width), F32),
        in_specs=[vmem] * 2,
        out_specs=pl.BlockSpec(memory_space=pltpu.HBM),
        scratch_shapes=[pltpu.VMEM((cols, width), F32), pltpu.SemaphoreType.DMA((cols // 256 + 1,))],
        compiler_params=pltpu.CompilerParams(vmem_limit_bytes=40 * 2**20),
        cost_estimate=pl.CostEstimate(flops=2 * tokens * width * cols, bytes_accessed=4 * width * cols,
                                      transcendentals=0),
        name="weight_grad",
    )(x_full, gt_blk)


def solution(mesh):
    n = mesh.shape["tp"]

    def per_device(x_blk, w_blk, grad_blk):
        x_full, gt_blk, own, plus, minus = exchange(x_blk, w_blk.T, grad_blk.T, n)
        from_left = lax.ppermute(plus, "tp", [(i, (i + 2) % n) for i in range(n)])
        from_right = lax.ppermute(minus, "tp", [(i, (i + n - 2) % n) for i in range(n)])
        grad_w = weight_grad(x_full, gt_blk).T
        grad_x = (own + from_left + from_right).astype(BF16)
        return grad_x, grad_w

    return jax.shard_map(
        per_device,
        mesh=mesh,
        in_specs=(P(("dp", "tp"), None), P(None, "tp"), P("dp", "tp")),
        out_specs=(P(("dp", "tp"), None), P("dp", "tp")),
        check_vma=False,
    )
```

time: 37 us -> 37.9 us (1.024)
  Pallas kernels: 32.2 us -> 33.1 us
    pallas_call x1, Pallas kernels: 20.3 us -> 21.2 us  [exchange(): pl.pallas_call(functools.partial(exchange_kernel, n), out_shape=(pltpu.VM...]
where the time goes in v3:
time: 37.9 us
  Pallas kernels  33.1 us (87%)
  starting transfers between devices  3.31 us (9%)
  other arithmetic  0.76 us (2%)
  between operations  0.66 us (2%)
    pallas_call x1, Pallas kernels, exchange(): pl.pallas_call(functools.partial(exchange_kernel, n), out_shape=(pltpu.VM...  21.2 us
    pallas_call x1, Pallas kernels, weight_grad(): pl.pallas_call(weight_kernel, out_shape=jax.ShapeDtypeStruct((cols, width...  11.9 us
    ppermute x1, starting transfers between devices, per_device(): lax.ppermute(minus, 'tp', [(i, (i + n - 2) % n) for i in range(n)])  2.36 us
    ppermute x1, starting transfers between devices, per_device(): from_left = lax.ppermute(plus, 'tp', [(i, (i + 2) % n) for i in range(n)])  0.96 us
  transfers between devices with their start and end apart: 2, of which 0 were waited for; matrix products, arithmetic and copies ran while one was open for 0% of the time, Pallas kernels for 32%

profile of v3, /device:TPU:112, one launch (start us, length us, event | category | flops | bytes accessed | tf_op | source)
XLA Modules:
  0.0 37.9 jit_solution(9331274238271874084)
XLA Ops:
  0.6 21.2 %exchange.1 = (bf16[256,3584]{1,0:T(8,128)(2,1)S(1)}, bf16[2368,256]{1,0:T(8,128)(2,1)S(1)}, f32[32,3584]{1,0:T(8,128)S(1)}, f32[32,3584]{1,0:T(8,128)S(1)}, f32[32,3584]{1,0:T(8,128)S(1)}) custom-call(bf16[32,3584]{1,0:T(8,128)(2,1)} %x_hbm.1, bf16[2368,3584]{1,0:T(8,128)(2,1)} %bitcast.4, bf16[2368,256]{1,0:T(8,128)(2,1)} %bitcast.5), custom_call_target="tpu_custom_call" | custom-call | flops 4345298944 | bytes 16973824 | tf_op jit(solution)/shard_map/exchange/pallas_call | solution.py:180
  21.8 1.0 %collective-permute-start = (f32[32,3584]{1,0:T(8,128)S(1)}, f32[32,3584]{1,0:T(8,128)S(1)}, u32[]{:S(2)}, u32[]{:S(2)}) collective-permute-start(f32[32,3584]{1,0:T(8,128)S(1)} %get-tuple-element.8), channel_id=1, source_target_pairs={{0,2},{1,3},{2,4},{3,5},{4,6},{5,7},{6,0},{7,1},{8,10},{9,11},{10,... | collective-permute-start | bytes 1376264 | tf_op jit(solution)/shard_map/ppermute | solution.py:265
  22.8 2.4 %collective-permute-start.1 = (f32[32,3584]{1,0:T(8,128)S(1)}, f32[32,3584]{1,0:T(8,128)S(1)}, u32[]{:S(2)}, u32[]{:S(2)}) collective-permute-start(f32[32,3584]{1,0:T(8,128)S(1)} %get-tuple-element.9), channel_id=1, source_target_pairs={{0,6},{1,7},{2,0},{3,1},{4,2},{5,3},{6,4},{7,5},{8,14},{9,15},{10,... | collective-permute-start | bytes 1376264 | tf_op jit(solution)/shard_map/ppermute | solution.py:266
  25.1 11.9 %weight_grad.1 = f32[2368,3584]{1,0:T(8,128)} custom-call(bf16[256,3584]{1,0:T(8,128)(2,1)S(1)} %get-tuple-element.10.x, bf16[2368,256]{1,0:T(8,128)(2,1)S(1)} %get-tuple-element.11.gt), custom_call_target="tpu_custom_call" | custom-call | flops 4345298944 | bytes 33947648 | tf_op jit(solution)/shard_map/weight_grad/pallas_call | solution.py:247
  37.1 0.0 collective-permute-done
  37.1 0.0 collective-permute-done.1
  37.1 0.8 %add_convert_fusion = bf16[32,3584]{1,0:T(8,128)(2,1)} fusion(f32[32,3584]{1,0:T(8,128)S(1)} %collective-permute-done.1, f32[32,3584]{1,0:T(8,128)S(1)} %get-tuple-element.7, f32[32,3584]{1,0:T(8,128)S(1)} %collective-permute-done), kind=kLoop, calls=%fused_computation | loop fusion | flops 344064 | bytes 1605632 | tf_op jit(solution)/shard_map/convert_element_type | solution.py:268
Async XLA Ops:
  21.8 15.3 %collective-permute-start = (f32[32,3584]{1,0:T(8,128)S(1)}, f32[32,3584]{1,0:T(8,128)S(1)}, u32[]{:S(2)}, u32[]{:S(2)}) collective-permute-start(f32[32,3584]{1,0:T(8,128)S(1)} %get-tuple-element.8), channel_id=1, source_target_pairs={{0,2},{1,3},{2,4},{3,5},{4,6},{5,7},{6,0},{7,1},{8,10},{9,11},{10,... | collective-permute-start | bytes 1376264 | tf_op jit(solution)/shard_map/ppermute | solution.py:265
  22.8 14.3 %collective-permute-start.1 = (f32[32,3584]{1,0:T(8,128)S(1)}, f32[32,3584]{1,0:T(8,128)S(1)}, u32[]{:S(2)}, u32[]{:S(2)}) collective-permute-start(f32[32,3584]{1,0:T(8,128)S(1)} %get-tuple-element.9), channel_id=1, source_target_pairs={{0,6},{1,7},{2,0},{3,1},{4,2},{5,3},{6,4},{7,5},{8,14},{9,15},{10,... | collective-permute-start | bytes 1376264 | tf_op jit(solution)/shard_map/ppermute | solution.py:266

commit v4 on v2

--- a/solution.py
+++ b/solution.py
@@ -90,8 +90,10 @@
             w_load(j + ahead).start()
         cols = pl.ds(j * blk, blk)
         t = jnp.dot(g[...], wbuf[:, cols], preferred_element_type=F32)
-        part[:, :, :, cols] = t.reshape(chips, 2, rows, blk)
-        d2d[j] = send(part.at[:, 1 - core, :, cols], rbuf.at[:, :, cols], d_send.at[j], d_recv.at[j], peer)
+        t = t.reshape(chips, 2, rows, blk)
+        for c in range(2):
+            part[j, c] = t[:, c]
+        d2d[j] = send(part.at[j, 1 - core], rbuf.at[j], d_send.at[j], d_recv.at[j], peer)
 
     u1 = []
 
@@ -99,14 +101,14 @@
         for j in js:
             cols = pl.ds(j * blk, blk)
             d2d[j].wait_recv()
-            opp_sum[:, cols] = part[c_opp, core, :, cols] + rbuf[c_opp, :, cols]
-            own[:, cols] = part[chip, core, :, cols] + rbuf[chip, :, cols]
-            plus[:, cols] = part[c_right, core, :, cols] + rbuf[c_right, :, cols]
-            minus[:, cols] = part[c_left, core, :, cols] + rbuf[c_left, :, cols]
-        cols = pl.ds(js[0] * blk, len(js) * blk)
+            opp_sum[j] = part[j, core, c_opp] + rbuf[j, c_opp]
+            own[:, cols] = part[j, core, chip] + rbuf[j, chip]
+            plus[:, cols] = part[j, core, c_right] + rbuf[j, c_right]
+            minus[:, cols] = part[j, core, c_left] + rbuf[j, c_left]
+        g0 = pl.ds(js[0], len(js))
         k = len(u1)
-        u1.append((js, send(opp_sum.at[lo, cols], u1buf.at[lo, cols], u_send.at[0, k], u_recv.at[0, k], right),
-                   send(opp_sum.at[hi, cols], u1buf.at[hi, cols], u_send.at[1, k], u_recv.at[1, k], left)))
+        u1.append((js, send(opp_sum.at[g0, lo], u1buf.at[g0, lo], u_send.at[0, k], u_recv.at[0, k], right),
+                   send(opp_sum.at[g0, hi], u1buf.at[g0, hi], u_send.at[1, k], u_recv.at[1, k], left)))
 
     for j in range(4):
         partial(j)
@@ -123,11 +125,12 @@
     arrived(4, low(opp))
     arrived(5, high(opp))
     for js, from_left, from_right in u1:
-        cols = pl.ds(js[0] * blk, len(js) * blk)
         from_left.wait_recv()
-        plus[lo, cols] += u1buf[lo, cols]
         from_right.wait_recv()
-        minus[hi, cols] += u1buf[hi, cols]
+        for j in js:
+            cols = pl.ds(j * blk, blk)
+            plus[lo, cols] += u1buf[j, lo]
+            minus[hi, cols] += u1buf[j, hi]
     for cp in pr.values():
         cp.wait()
     for cp in ag.values():
@@ -156,10 +159,10 @@
         scratch_shapes=[
             pltpu.VMEM((cols, width), BF16),
             pltpu.VMEM((tokens, cols), BF16),
-            pltpu.VMEM((chips, 2, rows, width), F32),
-            pltpu.VMEM((chips, rows, width), F32),
-            pltpu.VMEM((rows, width), F32),
-            pltpu.VMEM((rows, width), F32),
+            pltpu.VMEM((nb, 2, chips, rows, width // nb), F32),
+            pltpu.VMEM((nb, chips, rows, width // nb), F32),
+            pltpu.VMEM((nb, rows, width // nb), F32),
+            pltpu.VMEM((nb, rows, width // nb), F32),
             pltpu.SemaphoreType.DMA,
             pltpu.SemaphoreType.DMA,
             pltpu.SemaphoreType.DMA((nb,)),

time: 37 us -> 37 us (level)
  no operation moved by 1% of the time
where the time goes in v4:
time: 37 us; the launch traced here: 36.9 us
  Pallas kernels  32.2 us (87%)
  starting transfers between devices  3.31 us (9%)
  other arithmetic  0.76 us (2%)
  between operations  0.66 us (2%)
    pallas_call x1, Pallas kernels, exchange(): pl.pallas_call(functools.partial(exchange_kernel, n, groups), out_shape=(...  20.3 us
    pallas_call x1, Pallas kernels, weight_grad(): pl.pallas_call(weight_kernel, out_shape=jax.ShapeDtypeStruct((cols, width...  11.9 us
    ppermute x1, starting transfers between devices, per_device(): lax.ppermute(minus, 'tp', [(i, (i + n - 2) % n) for i in range(n)])  2.42 us
    ppermute x1, starting transfers between devices, per_device(): from_left = lax.ppermute(plus, 'tp', [(i, (i + 2) % n) for i in range(n)])  0.89 us
    convert_element_type x1, other arithmetic, per_device(): grad_x = (own + from_left + from_right).astype(BF16)  0.76 us
  transfers between devices with their start and end apart: 2, of which 0 were waited for; matrix products, arithmetic and copies ran while one was open for 0% of the time, Pallas kernels for 32%

profile of v4, /device:TPU:112, one launch (start us, length us, event | category | flops | bytes accessed | tf_op | source)
XLA Modules:
  0.0 36.9 jit_solution(2056319598867978786)
XLA Ops:
  0.6 20.3 %exchange.1 = (bf16[256,3584]{1,0:T(8,128)(2,1)S(1)}, bf16[2368,256]{1,0:T(8,128)(2,1)S(1)}, f32[32,3584]{1,0:T(8,128)S(1)}, f32[32,3584]{1,0:T(8,128)S(1)}, f32[32,3584]{1,0:T(8,128)S(1)}) custom-call(bf16[32,3584]{1,0:T(8,128)(2,1)} %x_hbm.1, bf16[2368,3584]{1,0:T(8,128)(2,1)} %bitcast.4, bf16[2368,256]{1,0:T(8,128)(2,1)} %bitcast.5), custom_call_target="tpu_custom_call" | custom-call | flops 4345298944 | bytes 16973824 | tf_op jit(solution)/shard_map/exchange/pallas_call | solution.py:154
  21.0 0.9 %collective-permute-start = (f32[32,3584]{1,0:T(8,128)S(1)}, f32[32,3584]{1,0:T(8,128)S(1)}, u32[]{:S(2)}, u32[]{:S(2)}) collective-permute-start(f32[32,3584]{1,0:T(8,128)S(1)} %get-tuple-element.8), channel_id=1, source_target_pairs={{0,2},{1,3},{2,4},{3,5},{4,6},{5,7},{6,0},{7,1},{8,10},{9,11},{10,... | collective-permute-start | bytes 1376264 | tf_op jit(solution)/shard_map/ppermute | solution.py:223
  21.8 2.4 %collective-permute-start.1 = (f32[32,3584]{1,0:T(8,128)S(1)}, f32[32,3584]{1,0:T(8,128)S(1)}, u32[]{:S(2)}, u32[]{:S(2)}) collective-permute-start(f32[32,3584]{1,0:T(8,128)S(1)} %get-tuple-element.9), channel_id=1, source_target_pairs={{0,6},{1,7},{2,0},{3,1},{4,2},{5,3},{6,4},{7,5},{8,14},{9,15},{10,... | collective-permute-start | bytes 1376264 | tf_op jit(solution)/shard_map/ppermute | solution.py:224
  24.3 11.9 %weight_grad.1 = f32[2368,3584]{1,0:T(8,128)} custom-call(bf16[256,3584]{1,0:T(8,128)(2,1)S(1)} %get-tuple-element.10.x, bf16[2368,256]{1,0:T(8,128)(2,1)S(1)} %get-tuple-element.11.gt), custom_call_target="tpu_custom_call" | custom-call | flops 4345298944 | bytes 33947648 | tf_op jit(solution)/shard_map/weight_grad/pallas_call | solution.py:205
  36.1 0.0 collective-permute-done
  36.2 0.0 collective-permute-done.1
  36.2 0.8 %add_convert_fusion = bf16[32,3584]{1,0:T(8,128)(2,1)} fusion(f32[32,3584]{1,0:T(8,128)S(1)} %collective-permute-done.1, f32[32,3584]{1,0:T(8,128)S(1)} %get-tuple-element.7, f32[32,3584]{1,0:T(8,128)S(1)} %collective-permute-done), kind=kLoop, calls=%fused_computation | loop fusion | flops 344064 | bytes 1605632 | tf_op jit(solution)/shard_map/convert_element_type | solution.py:226
Async XLA Ops:
  21.0 15.2 %collective-permute-start = (f32[32,3584]{1,0:T(8,128)S(1)}, f32[32,3584]{1,0:T(8,128)S(1)}, u32[]{:S(2)}, u32[]{:S(2)}) collective-permute-start(f32[32,3584]{1,0:T(8,128)S(1)} %get-tuple-element.8), channel_id=1, source_target_pairs={{0,2},{1,3},{2,4},{3,5},{4,6},{5,7},{6,0},{7,1},{8,10},{9,11},{10,... | collective-permute-start | bytes 1376264 | tf_op jit(solution)/shard_map/ppermute | solution.py:223
  21.8 14.3 %collective-permute-start.1 = (f32[32,3584]{1,0:T(8,128)S(1)}, f32[32,3584]{1,0:T(8,128)S(1)}, u32[]{:S(2)}, u32[]{:S(2)}) collective-permute-start(f32[32,3584]{1,0:T(8,128)S(1)} %get-tuple-element.9), channel_id=1, source_target_pairs={{0,6},{1,7},{2,0},{3,1},{4,2},{5,3},{6,4},{7,5},{8,14},{9,15},{10,... | collective-permute-start | bytes 1376264 | tf_op jit(solution)/shard_map/ppermute | solution.py:224

commit v5 on v4

--- a/solution.py
+++ b/solution.py
@@ -64,19 +64,17 @@
 
     own_x.wait()
     ag = {}
-    ag[0] = send(low(me), low(me), ag_send.at[0], ag_recv.at[0], right)
-    ag[3] = send(high(me), high(me), ag_send.at[3], ag_recv.at[3], left)
-    ag[1] = send(high(me), high(me), ag_send.at[1], ag_recv.at[1], right)
-    ag[2] = send(low(me), low(me), ag_send.at[2], ag_recv.at[2], left)
+    ag[0] = send(at(me), at(me), ag_send.at[0], ag_recv.at[0], right)
+    ag[1] = send(at(me), at(me), ag_send.at[1], ag_recv.at[1], left)
     pr = {}
-    pr[6] = send(at(me), at(me), pr_send.at[6], pr_recv.at[6], peer)
+    pr[4] = send(at(me), at(me), pr_send.at[4], pr_recv.at[4], peer)
 
     def arrived(slot, block, onward=None):
         pltpu.make_async_remote_copy(src_ref=block, dst_ref=block, send_sem=ag_send.at[slot],
                                      recv_sem=ag_recv.at[slot], device_id={"tp": me}, device_id_type=MESH).wait_recv()
         if onward is not None:
-            to, dev = onward
-            ag[to] = send(block, block, ag_send.at[to], ag_recv.at[to], dev)
+            to, piece, dev = onward
+            ag[to] = send(piece, piece, ag_send.at[to], ag_recv.at[to], dev)
         pr[slot] = send(block, block, pr_send.at[slot], pr_recv.at[slot], peer)
 
     g_load.wait()
@@ -110,20 +108,16 @@
         u1.append((js, send(opp_sum.at[g0, lo], u1buf.at[g0, lo], u_send.at[0, k], u_recv.at[0, k], right),
                    send(opp_sum.at[g0, hi], u1buf.at[g0, hi], u_send.at[1, k], u_recv.at[1, k], left)))
 
-    for j in range(4):
+    for j in range(5):
         partial(j)
-    arrived(0, low(left), (4, right))
-    arrived(3, high(right), (5, left))
     chip_sum(groups[0])
-    partial(4)
-    arrived(1, high(left))
-    arrived(2, low(right))
     partial(5)
     partial(6)
+    arrived(0, at(left), (2, low(left), right))
+    arrived(1, at(right), (3, high(right), left))
     chip_sum(groups[1])
-    chip_sum(groups[2])
-    arrived(4, low(opp))
-    arrived(5, high(opp))
+    arrived(2, low(opp))
+    arrived(3, high(opp))
     for js, from_left, from_right in u1:
         from_left.wait_recv()
         from_right.wait_recv()
@@ -147,7 +141,7 @@
     cols, tokens = gt_blk.shape
     chips = n // 2
     nb = 7
-    groups = ((0, 1, 2, 3), (4, 5), (6,))
+    groups = ((0, 1, 2, 3), (4, 5, 6))
     hbm = pl.BlockSpec(memory_space=pltpu.HBM)
     vmem = pl.BlockSpec(memory_space=pltpu.VMEM)
     part = pltpu.VMEM((rows, width), F32)
@@ -166,10 +160,10 @@
             pltpu.SemaphoreType.DMA,
             pltpu.SemaphoreType.DMA,
             pltpu.SemaphoreType.DMA((nb,)),
-            pltpu.SemaphoreType.DMA((6,)),
-            pltpu.SemaphoreType.DMA((6,)),
-            pltpu.SemaphoreType.DMA((7,)),
-            pltpu.SemaphoreType.DMA((7,)),
+            pltpu.SemaphoreType.DMA((4,)),
+            pltpu.SemaphoreType.DMA((4,)),
+            pltpu.SemaphoreType.DMA((5,)),
+            pltpu.SemaphoreType.DMA((5,)),
             pltpu.SemaphoreType.DMA((nb,)),
             pltpu.SemaphoreType.DMA((nb,)),
             pltpu.SemaphoreType.DMA((2, len(groups))),
@@ -183,15 +177,15 @@
 
 
 def weight_kernel(x, gt, o_hbm, obuf, o_sem):
-    cols = gt.shape[0]
+    cols, width = o_hbm.shape
     blk = 256
-    starts = ([0] if cols % blk else []) + list(range(cols % blk, cols, blk))
-    ends = starts[1:] + [cols]
+    pieces = [(0, blk, c, min(512, width - c)) for c in range(0, width, 512)]
+    pieces += [(r, min(blk, cols - r), 0, width) for r in range(blk, cols, blk)]
     stores = []
-    for i, (a, b) in enumerate(zip(starts, ends)):
-        r = pl.ds(a, b - a)
-        obuf[r, :] = jnp.dot(gt[r, :], x[...], preferred_element_type=F32)
-        cp = pltpu.make_async_copy(obuf.at[r, :], o_hbm.at[r, :], o_sem.at[i])
+    for i, (r, nr, c, nc) in enumerate(pieces):
+        rs, cs = pl.ds(r, nr), pl.ds(c, nc)
+        obuf[rs, cs] = jnp.dot(gt[rs, :], x[:, cs], preferred_element_type=F32)
+        cp = pltpu.make_async_copy(obuf.at[rs, cs], o_hbm.at[rs, cs], o_sem.at[i])
         cp.start()
         stores.append(cp)
     for cp in stores:
@@ -207,7 +201,7 @@
         out_shape=jax.ShapeDtypeStruct((cols, width), F32),
         in_specs=[vmem] * 2,
         out_specs=pl.BlockSpec(memory_space=pltpu.HBM),
-        scratch_shapes=[pltpu.VMEM((cols, width), F32), pltpu.SemaphoreType.DMA((16,))],
+        scratch_shapes=[pltpu.VMEM((cols, width), F32), pltpu.SemaphoreType.DMA((pl.cdiv(width, 512) + pl.cdiv(cols, 256),))],
         compiler_params=pltpu.CompilerParams(vmem_limit_bytes=40 * 2**20),
         cost_estimate=pl.CostEstimate(flops=2 * tokens * width * cols, bytes_accessed=4 * width * cols,
                                       transcendentals=0),

time: 37 us -> 37 us (level)
    ppermute x1, starting transfers between devices: 2.42 us -> 3.13 us  [per_device(): lax.ppermute(minus, 'tp', [(i, (i + n - 2) % n) for i in range(n)])]
    ppermute x1, starting transfers between devices: 0.89 us -> 0.19 us  [per_device(): from_left = lax.ppermute(plus, 'tp', [(i, (i + 2) % n) for i in range(n)])]
    pallas_call x1, Pallas kernels: 11.9 us -> 11.4 us  [weight_grad(): pl.pallas_call(weight_kernel, out_shape=jax.ShapeDtypeStruct((cols, width...]
    pallas_call x1, Pallas kernels: 20.3 us -> 20.7 us  [exchange(): pl.pallas_call(functools.partial(exchange_kernel, n, groups), out_shape=(...]
  transfers between devices with their start and end apart: 2 -> 2, of which waited for: 0 -> 0; matrix products, arithmetic and copies ran while one was open for 0% -> 0% of each run, Pallas kernels for 32% -> 31%
where the time goes in v5:
time: 37 us; the launch traced here: 36.9 us
  Pallas kernels  32.2 us (87%)
  starting transfers between devices  3.31 us (9%)
  other arithmetic  0.76 us (2%)
  between operations  0.66 us (2%)
    pallas_call x1, Pallas kernels, exchange(): pl.pallas_call(functools.partial(exchange_kernel, n, groups), out_shape=(...  20.7 us
    pallas_call x1, Pallas kernels, weight_grad(): pl.pallas_call(weight_kernel, out_shape=jax.ShapeDtypeStruct((cols, width...  11.4 us
    ppermute x1, starting transfers between devices, per_device(): lax.ppermute(minus, 'tp', [(i, (i + n - 2) % n) for i in range(n)])  3.13 us
    convert_element_type x1, other arithmetic, per_device(): grad_x = (own + from_left + from_right).astype(BF16)  0.76 us
  transfers between devices with their start and end apart: 2, of which 0 were waited for; matrix products, arithmetic and copies ran while one was open for 0% of the time, Pallas kernels for 31%

profile of v5, /device:TPU:112, one launch (start us, length us, event | category | flops | bytes accessed | tf_op | source)
XLA Modules:
  0.0 36.9 jit_solution(15256938468830995972)
XLA Ops:
  0.6 20.7 %exchange.1 = (bf16[256,3584]{1,0:T(8,128)(2,1)S(1)}, bf16[2368,256]{1,0:T(8,128)(2,1)S(1)}, f32[32,3584]{1,0:T(8,128)S(1)}, f32[32,3584]{1,0:T(8,128)S(1)}, f32[32,3584]{1,0:T(8,128)S(1)}) custom-call(bf16[32,3584]{1,0:T(8,128)(2,1)} %x_hbm.1, bf16[2368,3584]{1,0:T(8,128)(2,1)} %bitcast.4, bf16[2368,256]{1,0:T(8,128)(2,1)} %bitcast.5), custom_call_target="tpu_custom_call" | custom-call | flops 4345298944 | bytes 16973824 | tf_op jit(solution)/shard_map/exchange/pallas_call | solution.py:148
  21.3 0.2 collective-permute-start
  21.5 3.1 %collective-permute-start.1 = (f32[32,3584]{1,0:T(8,128)S(1)}, f32[32,3584]{1,0:T(8,128)S(1)}, u32[]{:S(2)}, u32[]{:S(2)}) collective-permute-start(f32[32,3584]{1,0:T(8,128)S(1)} %get-tuple-element.9), channel_id=1, source_target_pairs={{0,6},{1,7},{2,0},{3,1},{4,2},{5,3},{6,4},{7,5},{8,14},{9,15},{10,... | collective-permute-start | bytes 1376264 | tf_op jit(solution)/shard_map/ppermute | solution.py:218
  24.7 11.4 %weight_grad.1 = f32[2368,3584]{1,0:T(8,128)} custom-call(bf16[256,3584]{1,0:T(8,128)(2,1)S(1)} %get-tuple-element.10.x, bf16[2368,256]{1,0:T(8,128)(2,1)S(1)} %get-tuple-element.11.gt), custom_call_target="tpu_custom_call" | custom-call | flops 4345298944 | bytes 33947648 | tf_op jit(solution)/shard_map/weight_grad/pallas_call | solution.py:199
  36.1 0.0 collective-permute-done
  36.1 0.0 collective-permute-done.1
  36.1 0.8 %add_convert_fusion = bf16[32,3584]{1,0:T(8,128)(2,1)} fusion(f32[32,3584]{1,0:T(8,128)S(1)} %collective-permute-done.1, f32[32,3584]{1,0:T(8,128)S(1)} %get-tuple-element.7, f32[32,3584]{1,0:T(8,128)S(1)} %collective-permute-done), kind=kLoop, calls=%fused_computation | loop fusion | flops 344064 | bytes 1605632 | tf_op jit(solution)/shard_map/convert_element_type | solution.py:220
Async XLA Ops:
  21.3 14.8 %collective-permute-start = (f32[32,3584]{1,0:T(8,128)S(1)}, f32[32,3584]{1,0:T(8,128)S(1)}, u32[]{:S(2)}, u32[]{:S(2)}) collective-permute-start(f32[32,3584]{1,0:T(8,128)S(1)} %get-tuple-element.8), channel_id=1, source_target_pairs={{0,2},{1,3},{2,4},{3,5},{4,6},{5,7},{6,0},{7,1},{8,10},{9,11},{10,... | collective-permute-start | bytes 1376264 | tf_op jit(solution)/shard_map/ppermute | solution.py:217
  21.5 14.6 %collective-permute-start.1 = (f32[32,3584]{1,0:T(8,128)S(1)}, f32[32,3584]{1,0:T(8,128)S(1)}, u32[]{:S(2)}, u32[]{:S(2)}) collective-permute-start(f32[32,3584]{1,0:T(8,128)S(1)} %get-tuple-element.9), channel_id=1, source_target_pairs={{0,6},{1,7},{2,0},{3,1},{4,2},{5,3},{6,4},{7,5},{8,14},{9,15},{10,... | collective-permute-start | bytes 1376264 | tf_op jit(solution)/shard_map/ppermute | solution.py:218

commit v6 on v5

--- a/solution.py
+++ b/solution.py
@@ -12,7 +12,7 @@
 BF16 = jnp.bfloat16
 
 
-def exchange_kernel(n, groups, x_hbm, wt_hbm, gt_hbm, xf, gt, own, plus, minus,
+def exchange_kernel(n, groups, x_hbm, wt_hbm, gt_hbm, xf, gt, own, first, second,
                     wbuf, g, part, rbuf, opp_sum, u1buf,
                     x_sem, g_sem, w_sem, ag_send, ag_recv, pr_send, pr_recv,
                     d_send, d_recv, u_send, u_recv):
@@ -28,6 +28,11 @@
     right, left, opp = 2 * c_right + core, 2 * c_left + core, 2 * c_opp + core
     peer = 2 * chip + 1 - core
     lo, hi = pl.ds(0, half), pl.ds(half, half)
+    odd = lax.rem(chip, 2)
+    c_first = odd * c_right + (1 - odd) * c_left
+    c_second = odd * c_left + (1 - odd) * c_right
+    r_first = pl.multiple_of((1 - odd) * half, half)
+    r_second = pl.multiple_of(odd * half, half)
 
     def at(dev, part_of=0, size=rows):
         return xf.at[pl.ds(pl.multiple_of(dev * rows + part_of * half, half), size), :]
@@ -101,8 +106,8 @@
             d2d[j].wait_recv()
             opp_sum[j] = part[j, core, c_opp] + rbuf[j, c_opp]
             own[:, cols] = part[j, core, chip] + rbuf[j, chip]
-            plus[:, cols] = part[j, core, c_right] + rbuf[j, c_right]
-            minus[:, cols] = part[j, core, c_left] + rbuf[j, c_left]
+            first[:, cols] = part[j, core, c_first] + rbuf[j, c_first]
+            second[:, cols] = part[j, core, c_second] + rbuf[j, c_second]
         g0 = pl.ds(js[0], len(js))
         k = len(u1)
         u1.append((js, send(opp_sum.at[g0, lo], u1buf.at[g0, lo], u_send.at[0, k], u_recv.at[0, k], right),
@@ -123,8 +128,8 @@
         from_right.wait_recv()
         for j in js:
             cols = pl.ds(j * blk, blk)
-            plus[lo, cols] += u1buf[j, lo]
-            minus[hi, cols] += u1buf[j, hi]
+            first[pl.ds(r_first, half), cols] += u1buf[j, pl.ds(r_first, half)]
+            second[pl.ds(r_second, half), cols] += u1buf[j, pl.ds(r_second, half)]
     for cp in pr.values():
         cp.wait()
     for cp in ag.values():
@@ -213,11 +218,20 @@
     n = mesh.shape["tp"]
 
     def per_device(x_blk, w_blk, grad_blk):
-        x_full, gt_blk, own, plus, minus = exchange(x_blk, w_blk.T, grad_blk.T, n)
-        from_left = lax.ppermute(plus, "tp", [(i, (i + 2) % n) for i in range(n)])
-        from_right = lax.ppermute(minus, "tp", [(i, (i + n - 2) % n) for i in range(n)])
+        x_full, gt_blk, own, first, second = exchange(x_blk, w_blk.T, grad_blk.T, n)
+
+        def swap(part, start):
+            pairs = []
+            for c in range(start, start + n // 2, 2):
+                for core in range(2):
+                    a, b = (2 * c + core) % n, (2 * c + 2 + core) % n
+                    pairs += [(a, b), (b, a)]
+            return lax.ppermute(part, "tp", pairs)
+
+        got_first = swap(first, 1)
+        got_second = swap(second, 0)
         grad_w = weight_grad(x_full, gt_blk).T
-        grad_x = (own + from_left + from_right).astype(BF16)
+        grad_x = (own + got_first + got_second).astype(BF16)
         return grad_x, grad_w
 
     return jax.shard_map(

time: 37 us -> 35.9 us (0.970)
  starting transfers between devices: 3.31 us -> 1.51 us
  waiting for transfers between devices: 0.01 us -> 0.76 us
    ppermute x2, starting transfers between devices: 3.31 us -> 1.51 us  [swap(): return lax.ppermute(part, 'tp', pairs)]
    ppermute x2, waiting for transfers between devices: 0.01 us -> 0.76 us  [swap(): return lax.ppermute(part, 'tp', pairs)]
  transfers between devices with their start and end apart: 2 -> 2, of which waited for: 0 -> 1; matrix products, arithmetic and copies ran while one was open for 0% -> 0% of each run, Pallas kernels for 31% -> 32%
where the time goes in v6:
time: 35.9 us; the launch traced here: 35.8 us
  Pallas kernels  32.2 us (90%)
  starting transfers between devices  1.51 us (4%)
  waiting for transfers between devices  0.76 us (2%)
  other arithmetic  0.76 us (2%)
  between operations  0.65 us (2%)
    pallas_call x1, Pallas kernels, exchange(): pl.pallas_call(functools.partial(exchange_kernel, n, groups), out_shape=(...  20.7 us
    pallas_call x1, Pallas kernels, weight_grad(): pl.pallas_call(weight_kernel, out_shape=jax.ShapeDtypeStruct((cols, width...  11.4 us
    ppermute x2, starting transfers between devices, swap(): return lax.ppermute(part, 'tp', pairs)  1.51 us
    ppermute x2, waiting for transfers between devices, swap(): return lax.ppermute(part, 'tp', pairs)  0.76 us
    convert_element_type x1, other arithmetic, per_device(): grad_x = (own + got_first + got_second).astype(BF16)  0.76 us
  transfers between devices with their start and end apart: 2, of which 1 were waited for; matrix products, arithmetic and copies ran while one was open for 0% of the time, Pallas kernels for 32%

profile of v6, /device:TPU:112, one launch (start us, length us, event | category | flops | bytes accessed | tf_op | source)
XLA Modules:
  0.0 35.8 jit_solution(12786370339100828676)
XLA Ops:
  0.6 20.7 %exchange.1 = (bf16[256,3584]{1,0:T(8,128)(2,1)S(1)}, bf16[2368,256]{1,0:T(8,128)(2,1)S(1)}, f32[32,3584]{1,0:T(8,128)S(1)}, f32[32,3584]{1,0:T(8,128)S(1)}, f32[32,3584]{1,0:T(8,128)S(1)}) custom-call(bf16[32,3584]{1,0:T(8,128)(2,1)} %x_hbm.1, bf16[2368,3584]{1,0:T(8,128)(2,1)} %bitcast.4, bf16[2368,256]{1,0:T(8,128)(2,1)} %bitcast.5), custom_call_target="tpu_custom_call" | custom-call | flops 4345298944 | bytes 16973824 | tf_op jit(solution)/shard_map/exchange/pallas_call | solution.py:153
  21.3 0.8 %collective-permute-start = (f32[32,3584]{1,0:T(8,128)S(1)}, f32[32,3584]{1,0:T(8,128)S(1)}, u32[]{:S(2)}, u32[]{:S(2)}) collective-permute-start(f32[32,3584]{1,0:T(8,128)S(1)} %get-tuple-element.8), channel_id=1, source_target_pairs={{2,4},{4,2},{3,5},{5,3},{6,0},{0,6},{7,1},{1,7},{10,12},{12,10},{1... | collective-permute-start | bytes 1376264 | tf_op jit(solution)/shard_map/ppermute | solution.py:229
  22.1 0.8 %collective-permute-start.1 = (f32[32,3584]{1,0:T(8,128)S(1)}, f32[32,3584]{1,0:T(8,128)S(1)}, u32[]{:S(2)}, u32[]{:S(2)}) collective-permute-start(f32[32,3584]{1,0:T(8,128)S(1)} %get-tuple-element.9), channel_id=1, source_target_pairs={{0,2},{2,0},{1,3},{3,1},{4,6},{6,4},{5,7},{7,5},{8,10},{10,8},{9,1... | collective-permute-start | bytes 1376264 | tf_op jit(solution)/shard_map/ppermute | solution.py:229
  22.9 11.4 %weight_grad.1 = f32[2368,3584]{1,0:T(8,128)} custom-call(bf16[256,3584]{1,0:T(8,128)(2,1)S(1)} %get-tuple-element.10.x, bf16[2368,256]{1,0:T(8,128)(2,1)S(1)} %get-tuple-element.11.gt), custom_call_target="tpu_custom_call" | custom-call | flops 4345298944 | bytes 33947648 | tf_op jit(solution)/shard_map/weight_grad/pallas_call | solution.py:204
  34.3 0.8 %collective-permute-done = f32[32,3584]{1,0:T(8,128)S(1)} collective-permute-done((f32[32,3584]{1,0:T(8,128)S(1)}, f32[32,3584]{1,0:T(8,128)S(1)}, u32[]{:S(2)}, u32[]{:S(2)}) %collective-permute-start) | collective-permute-done | bytes 458784 | tf_op jit(solution)/shard_map/ppermute | solution.py:229
  35.1 0.0 collective-permute-done.1
  35.1 0.8 %add_convert_fusion = bf16[32,3584]{1,0:T(8,128)(2,1)} fusion(f32[32,3584]{1,0:T(8,128)S(1)} %collective-permute-done.1, f32[32,3584]{1,0:T(8,128)S(1)} %get-tuple-element.7, f32[32,3584]{1,0:T(8,128)S(1)} %collective-permute-done), kind=kLoop, calls=%fused_computation | loop fusion | flops 344064 | bytes 1605632 | tf_op jit(solution)/shard_map/convert_element_type | solution.py:234
Async XLA Ops:
  21.3 13.7 %collective-permute-start = (f32[32,3584]{1,0:T(8,128)S(1)}, f32[32,3584]{1,0:T(8,128)S(1)}, u32[]{:S(2)}, u32[]{:S(2)}) collective-permute-start(f32[32,3584]{1,0:T(8,128)S(1)} %get-tuple-element.8), channel_id=1, source_target_pairs={{2,4},{4,2},{3,5},{5,3},{6,0},{0,6},{7,1},{1,7},{10,12},{12,10},{1... | collective-permute-start | bytes 1376264 | tf_op jit(solution)/shard_map/ppermute | solution.py:229
  22.1 13.0 %collective-permute-start.1 = (f32[32,3584]{1,0:T(8,128)S(1)}, f32[32,3584]{1,0:T(8,128)S(1)}, u32[]{:S(2)}, u32[]{:S(2)}) collective-permute-start(f32[32,3584]{1,0:T(8,128)S(1)} %get-tuple-element.9), channel_id=1, source_target_pairs={{0,2},{2,0},{1,3},{3,1},{4,6},{6,4},{5,7},{7,5},{8,10},{10,8},{9,1... | collective-permute-start | bytes 1376264 | tf_op jit(solution)/shard_map/ppermute | solution.py:229

commit v7 on v6

--- a/solution.py
+++ b/solution.py
@@ -113,14 +113,18 @@
         u1.append((js, send(opp_sum.at[g0, lo], u1buf.at[g0, lo], u_send.at[0, k], u_recv.at[0, k], right),
                    send(opp_sum.at[g0, hi], u1buf.at[g0, hi], u_send.at[1, k], u_recv.at[1, k], left)))
 
-    for j in range(5):
-        partial(j)
+    partial(0)
+    partial(1)
+    partial(2)
     chip_sum(groups[0])
+    partial(3)
+    partial(4)
+    chip_sum(groups[1])
     partial(5)
     partial(6)
     arrived(0, at(left), (2, low(left), right))
     arrived(1, at(right), (3, high(right), left))
-    chip_sum(groups[1])
+    chip_sum(groups[2])
     arrived(2, low(opp))
     arrived(3, high(opp))
     for js, from_left, from_right in u1:
@@ -146,7 +150,7 @@
     cols, tokens = gt_blk.shape
     chips = n // 2
     nb = 7
-    groups = ((0, 1, 2, 3), (4, 5, 6))
+    groups = ((0, 1), (2, 3), (4, 5, 6))
     hbm = pl.BlockSpec(memory_space=pltpu.HBM)
     vmem = pl.BlockSpec(memory_space=pltpu.VMEM)
     part = pltpu.VMEM((rows, width), F32)

time: 35.9 us -> 35.2 us (0.981)
  Pallas kernels: 32.2 us -> 31.7 us
    pallas_call x1, Pallas kernels: 20.7 us -> 20.2 us  [exchange(): pl.pallas_call(functools.partial(exchange_kernel, n, groups), out_shape=(...]
  transfers between devices with their start and end apart: 2 -> 2, of which waited for: 1 -> 1; matrix products, arithmetic and copies ran while one was open for 0% -> 0% of each run, Pallas kernels for 32% -> 33%
where the time goes in v7:
time: 35.2 us; the launch traced here: 35.1 us
  Pallas kernels  31.7 us (90%)
  starting transfers between devices  1.49 us (4%)
  other arithmetic  0.76 us (2%)
  between operations  0.65 us (2%)
  waiting for transfers between devices  0.53 us (2%)
    pallas_call x1, Pallas kernels, exchange(): pl.pallas_call(functools.partial(exchange_kernel, n, groups), out_shape=(...  20.2 us
    pallas_call x1, Pallas kernels, weight_grad(): pl.pallas_call(weight_kernel, out_shape=jax.ShapeDtypeStruct((cols, width...  11.4 us
    ppermute x2, starting transfers between devices, swap(): return lax.ppermute(part, 'tp', pairs)  1.49 us
    convert_element_type x1, other arithmetic, per_device(): grad_x = (own + got_first + got_second).astype(BF16)  0.76 us
  transfers between devices with their start and end apart: 2, of which 1 were waited for; matrix products, arithmetic and copies ran while one was open for 0% of the time, Pallas kernels for 33%

profile of v7, /device:TPU:112, one launch (start us, length us, event | category | flops | bytes accessed | tf_op | source)
XLA Modules:
  0.0 35.1 jit_solution(5381764924498265632)
XLA Ops:
  0.6 20.2 %exchange.1 = (bf16[256,3584]{1,0:T(8,128)(2,1)S(1)}, bf16[2368,256]{1,0:T(8,128)(2,1)S(1)}, f32[32,3584]{1,0:T(8,128)S(1)}, f32[32,3584]{1,0:T(8,128)S(1)}, f32[32,3584]{1,0:T(8,128)S(1)}) custom-call(bf16[32,3584]{1,0:T(8,128)(2,1)} %x_hbm.1, bf16[2368,3584]{1,0:T(8,128)(2,1)} %bitcast.4, bf16[2368,256]{1,0:T(8,128)(2,1)} %bitcast.5), custom_call_target="tpu_custom_call" | custom-call | flops 4345298944 | bytes 16973824 | tf_op jit(solution)/shard_map/exchange/pallas_call | solution.py:157
  20.9 0.8 %collective-permute-start = (f32[32,3584]{1,0:T(8,128)S(1)}, f32[32,3584]{1,0:T(8,128)S(1)}, u32[]{:S(2)}, u32[]{:S(2)}) collective-permute-start(f32[32,3584]{1,0:T(8,128)S(1)} %get-tuple-element.8), channel_id=1, source_target_pairs={{2,4},{4,2},{3,5},{5,3},{6,0},{0,6},{7,1},{1,7},{10,12},{12,10},{1... | collective-permute-start | bytes 1376264 | tf_op jit(solution)/shard_map/ppermute | solution.py:233
  21.6 0.7 %collective-permute-start.1 = (f32[32,3584]{1,0:T(8,128)S(1)}, f32[32,3584]{1,0:T(8,128)S(1)}, u32[]{:S(2)}, u32[]{:S(2)}) collective-permute-start(f32[32,3584]{1,0:T(8,128)S(1)} %get-tuple-element.9), channel_id=1, source_target_pairs={{0,2},{2,0},{1,3},{3,1},{4,6},{6,4},{5,7},{7,5},{8,10},{10,8},{9,1... | collective-permute-start | bytes 1376264 | tf_op jit(solution)/shard_map/ppermute | solution.py:233
  22.4 11.4 %weight_grad.1 = f32[2368,3584]{1,0:T(8,128)} custom-call(bf16[256,3584]{1,0:T(8,128)(2,1)S(1)} %get-tuple-element.10.x, bf16[2368,256]{1,0:T(8,128)(2,1)S(1)} %get-tuple-element.11.gt), custom_call_target="tpu_custom_call" | custom-call | flops 4345298944 | bytes 33947648 | tf_op jit(solution)/shard_map/weight_grad/pallas_call | solution.py:208
  33.8 0.5 %collective-permute-done = f32[32,3584]{1,0:T(8,128)S(1)} collective-permute-done((f32[32,3584]{1,0:T(8,128)S(1)}, f32[32,3584]{1,0:T(8,128)S(1)}, u32[]{:S(2)}, u32[]{:S(2)}) %collective-permute-start) | collective-permute-done | bytes 458784 | tf_op jit(solution)/shard_map/ppermute | solution.py:233
  34.4 0.0 collective-permute-done.1
  34.4 0.8 %add_convert_fusion = bf16[32,3584]{1,0:T(8,128)(2,1)} fusion(f32[32,3584]{1,0:T(8,128)S(1)} %collective-permute-done.1, f32[32,3584]{1,0:T(8,128)S(1)} %get-tuple-element.7, f32[32,3584]{1,0:T(8,128)S(1)} %collective-permute-done), kind=kLoop, calls=%fused_computation | loop fusion | flops 344064 | bytes 1605632 | tf_op jit(solution)/shard_map/convert_element_type | solution.py:238
Async XLA Ops:
  20.9 13.5 %collective-permute-start = (f32[32,3584]{1,0:T(8,128)S(1)}, f32[32,3584]{1,0:T(8,128)S(1)}, u32[]{:S(2)}, u32[]{:S(2)}) collective-permute-start(f32[32,3584]{1,0:T(8,128)S(1)} %get-tuple-element.8), channel_id=1, source_target_pairs={{2,4},{4,2},{3,5},{5,3},{6,0},{0,6},{7,1},{1,7},{10,12},{12,10},{1... | collective-permute-start | bytes 1376264 | tf_op jit(solution)/shard_map/ppermute | solution.py:233
  21.6 12.7 %collective-permute-start.1 = (f32[32,3584]{1,0:T(8,128)S(1)}, f32[32,3584]{1,0:T(8,128)S(1)}, u32[]{:S(2)}, u32[]{:S(2)}) collective-permute-start(f32[32,3584]{1,0:T(8,128)S(1)} %get-tuple-element.9), channel_id=1, source_target_pairs={{0,2},{2,0},{1,3},{3,1},{4,6},{6,4},{5,7},{7,5},{8,10},{10,8},{9,1... | collective-permute-start | bytes 1376264 | tf_op jit(solution)/shard_map/ppermute | solution.py:233

commit v8 on v7

--- a/solution.py
+++ b/solution.py
@@ -43,11 +43,15 @@
     def high(dev):
         return at(dev, 1, half)
 
+    barrier = pltpu.get_barrier_semaphore()
+    for dev in (left, right, peer):
+        pl.semaphore_signal(barrier, inc=1, device_id={"tp": dev}, device_id_type=MESH)
+
     own_x = pltpu.make_async_copy(x_hbm, at(me), x_sem)
     own_x.start()
     g_load = pltpu.make_async_copy(gt_hbm, gt, g_sem)
     g_load.start()
-    ahead = 3
+    ahead = 5
 
     def w_load(j):
         cols = pl.ds(j * blk, blk)
@@ -56,9 +60,6 @@
     for j in range(ahead):
         w_load(j).start()
 
-    barrier = pltpu.get_barrier_semaphore()
-    for dev in (left, right, peer):
-        pl.semaphore_signal(barrier, inc=1, device_id={"tp": dev}, device_id_type=MESH)
     pl.semaphore_wait(barrier, 3)
 
     def send(src, dst, s_sem, r_sem, dev):
@@ -127,13 +128,6 @@
     chip_sum(groups[2])
     arrived(2, low(opp))
     arrived(3, high(opp))
-    for js, from_left, from_right in u1:
-        from_left.wait_recv()
-        from_right.wait_recv()
-        for j in js:
-            cols = pl.ds(j * blk, blk)
-            first[pl.ds(r_first, half), cols] += u1buf[j, pl.ds(r_first, half)]
-            second[pl.ds(r_second, half), cols] += u1buf[j, pl.ds(r_second, half)]
     for cp in pr.values():
         cp.wait()
     for cp in ag.values():
@@ -143,6 +137,13 @@
     for _, a, b in u1:
         a.wait_send()
         b.wait_send()
+    for js, from_left, from_right in u1:
+        from_left.wait_recv()
+        from_right.wait_recv()
+        for j in js:
+            cols = pl.ds(j * blk, blk)
+            first[pl.ds(r_first, half), cols] += u1buf[j, pl.ds(r_first, half)]
+            second[pl.ds(r_second, half), cols] += u1buf[j, pl.ds(r_second, half)]
 
 
 def exchange(x_blk, wt_blk, gt_blk, n):

time: 35.2 us -> 36.7 us (1.043)
  Pallas kernels: 31.7 us -> 32.8 us
  waiting for transfers between devices: 0.53 us -> 0.96 us
    pallas_call x1, Pallas kernels: 20.2 us -> 21.3 us  [exchange(): pl.pallas_call(functools.partial(exchange_kernel, n, groups), out_shape=(...]
    ppermute x2, waiting for transfers between devices: 0.53 us -> 0.96 us  [swap(): return lax.ppermute(part, 'tp', pairs)]
  transfers between devices with their start and end apart: 2 -> 2, of which waited for: 1 -> 1; matrix products, arithmetic and copies ran while one was open for 0% -> 0% of each run, Pallas kernels for 33% -> 31%
where the time goes in v8:
time: 36.7 us
  Pallas kernels  32.8 us (89%)
  starting transfers between devices  1.51 us (4%)
  waiting for transfers between devices  0.96 us (3%)
  other arithmetic  0.76 us (2%)
  between operations  0.65 us (2%)
    pallas_call x1, Pallas kernels, exchange(): pl.pallas_call(functools.partial(exchange_kernel, n, groups), out_shape=(...  21.3 us
    pallas_call x1, Pallas kernels, weight_grad(): pl.pallas_call(weight_kernel, out_shape=jax.ShapeDtypeStruct((cols, width...  11.4 us
    ppermute x2, starting transfers between devices, swap(): return lax.ppermute(part, 'tp', pairs)  1.51 us
    ppermute x2, waiting for transfers between devices, swap(): return lax.ppermute(part, 'tp', pairs)  0.96 us
    convert_element_type x1, other arithmetic, per_device(): grad_x = (own + got_first + got_second).astype(BF16)  0.76 us
  transfers between devices with their start and end apart: 2, of which 1 were waited for; matrix products, arithmetic and copies ran while one was open for 0% of the time, Pallas kernels for 31%

profile of v8, /device:TPU:112, one launch (start us, length us, event | category | flops | bytes accessed | tf_op | source)
XLA Modules:
  0.0 36.7 jit_solution(5361193393657057201)
XLA Ops:
  0.6 21.3 %exchange.1 = (bf16[256,3584]{1,0:T(8,128)(2,1)S(1)}, bf16[2368,256]{1,0:T(8,128)(2,1)S(1)}, f32[32,3584]{1,0:T(8,128)S(1)}, f32[32,3584]{1,0:T(8,128)S(1)}, f32[32,3584]{1,0:T(8,128)S(1)}) custom-call(bf16[32,3584]{1,0:T(8,128)(2,1)} %x_hbm.1, bf16[2368,3584]{1,0:T(8,128)(2,1)} %bitcast.4, bf16[2368,256]{1,0:T(8,128)(2,1)} %bitcast.5), custom_call_target="tpu_custom_call" | custom-call | flops 4345298944 | bytes 16973824 | tf_op jit(solution)/shard_map/exchange/pallas_call | solution.py:158
  22.0 0.8 %collective-permute-start = (f32[32,3584]{1,0:T(8,128)S(1)}, f32[32,3584]{1,0:T(8,128)S(1)}, u32[]{:S(2)}, u32[]{:S(2)}) collective-permute-start(f32[32,3584]{1,0:T(8,128)S(1)} %get-tuple-element.8), channel_id=1, source_target_pairs={{2,4},{4,2},{3,5},{5,3},{6,0},{0,6},{7,1},{1,7},{10,12},{12,10},{1... | collective-permute-start | bytes 1376264 | tf_op jit(solution)/shard_map/ppermute | solution.py:234
  22.7 0.7 %collective-permute-start.1 = (f32[32,3584]{1,0:T(8,128)S(1)}, f32[32,3584]{1,0:T(8,128)S(1)}, u32[]{:S(2)}, u32[]{:S(2)}) collective-permute-start(f32[32,3584]{1,0:T(8,128)S(1)} %get-tuple-element.9), channel_id=1, source_target_pairs={{0,2},{2,0},{1,3},{3,1},{4,6},{6,4},{5,7},{7,5},{8,10},{10,8},{9,1... | collective-permute-start | bytes 1376264 | tf_op jit(solution)/shard_map/ppermute | solution.py:234
  23.5 11.4 %weight_grad.1 = f32[2368,3584]{1,0:T(8,128)} custom-call(bf16[256,3584]{1,0:T(8,128)(2,1)S(1)} %get-tuple-element.10.x, bf16[2368,256]{1,0:T(8,128)(2,1)S(1)} %get-tuple-element.11.gt), custom_call_target="tpu_custom_call" | custom-call | flops 4345298944 | bytes 33947648 | tf_op jit(solution)/shard_map/weight_grad/pallas_call | solution.py:209
  34.9 1.0 %collective-permute-done = f32[32,3584]{1,0:T(8,128)S(1)} collective-permute-done((f32[32,3584]{1,0:T(8,128)S(1)}, f32[32,3584]{1,0:T(8,128)S(1)}, u32[]{:S(2)}, u32[]{:S(2)}) %collective-permute-start) | collective-permute-done | bytes 458784 | tf_op jit(solution)/shard_map/ppermute | solution.py:234
  35.9 0.0 collective-permute-done.1
  35.9 0.8 %add_convert_fusion = bf16[32,3584]{1,0:T(8,128)(2,1)} fusion(f32[32,3584]{1,0:T(8,128)S(1)} %collective-permute-done.1, f32[32,3584]{1,0:T(8,128)S(1)} %get-tuple-element.7, f32[32,3584]{1,0:T(8,128)S(1)} %collective-permute-done), kind=kLoop, calls=%fused_computation | loop fusion | flops 344064 | bytes 1605632 | tf_op jit(solution)/shard_map/convert_element_type | solution.py:239
Async XLA Ops:
  22.0 13.9 %collective-permute-start = (f32[32,3584]{1,0:T(8,128)S(1)}, f32[32,3584]{1,0:T(8,128)S(1)}, u32[]{:S(2)}, u32[]{:S(2)}) collective-permute-start(f32[32,3584]{1,0:T(8,128)S(1)} %get-tuple-element.8), channel_id=1, source_target_pairs={{2,4},{4,2},{3,5},{5,3},{6,0},{0,6},{7,1},{1,7},{10,12},{12,10},{1... | collective-permute-start | bytes 1376264 | tf_op jit(solution)/shard_map/ppermute | solution.py:234
  22.7 13.2 %collective-permute-start.1 = (f32[32,3584]{1,0:T(8,128)S(1)}, f32[32,3584]{1,0:T(8,128)S(1)}, u32[]{:S(2)}, u32[]{:S(2)}) collective-permute-start(f32[32,3584]{1,0:T(8,128)S(1)} %get-tuple-element.9), channel_id=1, source_target_pairs={{0,2},{2,0},{1,3},{3,1},{4,6},{6,4},{5,7},{7,5},{8,10},{10,8},{9,1... | collective-permute-start | bytes 1376264 | tf_op jit(solution)/shard_map/ppermute | solution.py:234

commit v9 on v8

--- a/solution.py
+++ b/solution.py
@@ -51,7 +51,7 @@
     own_x.start()
     g_load = pltpu.make_async_copy(gt_hbm, gt, g_sem)
     g_load.start()
-    ahead = 5
+    ahead = 2
 
     def w_load(j):
         cols = pl.ds(j * blk, blk)

time: 36.7 us -> 35.3 us (0.962)
  Pallas kernels: 32.8 us -> 31.7 us
  waiting for transfers between devices: 0.96 us -> 0.59 us
    pallas_call x1, Pallas kernels: 21.3 us -> 20.3 us  [exchange(): pl.pallas_call(functools.partial(exchange_kernel, n, groups), out_shape=(...]
  transfers between devices with their start and end apart: 2 -> 2, of which waited for: 1 -> 1; matrix products, arithmetic and copies ran while one was open for 0% -> 0% of each run, Pallas kernels for 31% -> 33%
where the time goes in v9:
time: 35.3 us; the launch traced here: 35.2 us
  Pallas kernels  31.7 us (90%)
  starting transfers between devices  1.49 us (4%)
  other arithmetic  0.76 us (2%)
  between operations  0.65 us (2%)
  waiting for transfers between devices  0.59 us (2%)
    pallas_call x1, Pallas kernels, exchange(): pl.pallas_call(functools.partial(exchange_kernel, n, groups), out_shape=(...  20.3 us
    pallas_call x1, Pallas kernels, weight_grad(): pl.pallas_call(weight_kernel, out_shape=jax.ShapeDtypeStruct((cols, width...  11.4 us
    ppermute x2, starting transfers between devices, swap(): return lax.ppermute(part, 'tp', pairs)  1.49 us
    convert_element_type x1, other arithmetic, per_device(): grad_x = (own + got_first + got_second).astype(BF16)  0.76 us
  transfers between devices with their start and end apart: 2, of which 1 were waited for; matrix products, arithmetic and copies ran while one was open for 0% of the time, Pallas kernels for 33%

profile of v9, /device:TPU:112, one launch (start us, length us, event | category | flops | bytes accessed | tf_op | source)
XLA Modules:
  0.0 35.2 jit_solution(914699345998563778)
XLA Ops:
  0.6 20.3 %exchange.1 = (bf16[256,3584]{1,0:T(8,128)(2,1)S(1)}, bf16[2368,256]{1,0:T(8,128)(2,1)S(1)}, f32[32,3584]{1,0:T(8,128)S(1)}, f32[32,3584]{1,0:T(8,128)S(1)}, f32[32,3584]{1,0:T(8,128)S(1)}) custom-call(bf16[32,3584]{1,0:T(8,128)(2,1)} %x_hbm.1, bf16[2368,3584]{1,0:T(8,128)(2,1)} %bitcast.4, bf16[2368,256]{1,0:T(8,128)(2,1)} %bitcast.5), custom_call_target="tpu_custom_call" | custom-call | flops 4345298944 | bytes 16973824 | tf_op jit(solution)/shard_map/exchange/pallas_call | solution.py:158
  20.9 0.8 %collective-permute-start = (f32[32,3584]{1,0:T(8,128)S(1)}, f32[32,3584]{1,0:T(8,128)S(1)}, u32[]{:S(2)}, u32[]{:S(2)}) collective-permute-start(f32[32,3584]{1,0:T(8,128)S(1)} %get-tuple-element.8), channel_id=1, source_target_pairs={{2,4},{4,2},{3,5},{5,3},{6,0},{0,6},{7,1},{1,7},{10,12},{12,10},{1... | collective-permute-start | bytes 1376264 | tf_op jit(solution)/shard_map/ppermute | solution.py:234
  21.7 0.7 %collective-permute-start.1 = (f32[32,3584]{1,0:T(8,128)S(1)}, f32[32,3584]{1,0:T(8,128)S(1)}, u32[]{:S(2)}, u32[]{:S(2)}) collective-permute-start(f32[32,3584]{1,0:T(8,128)S(1)} %get-tuple-element.9), channel_id=1, source_target_pairs={{0,2},{2,0},{1,3},{3,1},{4,6},{6,4},{5,7},{7,5},{8,10},{10,8},{9,1... | collective-permute-start | bytes 1376264 | tf_op jit(solution)/shard_map/ppermute | solution.py:234
  22.4 11.4 %weight_grad.1 = f32[2368,3584]{1,0:T(8,128)} custom-call(bf16[256,3584]{1,0:T(8,128)(2,1)S(1)} %get-tuple-element.10.x, bf16[2368,256]{1,0:T(8,128)(2,1)S(1)} %get-tuple-element.11.gt), custom_call_target="tpu_custom_call" | custom-call | flops 4345298944 | bytes 33947648 | tf_op jit(solution)/shard_map/weight_grad/pallas_call | solution.py:209
  33.9 0.6 %collective-permute-done = f32[32,3584]{1,0:T(8,128)S(1)} collective-permute-done((f32[32,3584]{1,0:T(8,128)S(1)}, f32[32,3584]{1,0:T(8,128)S(1)}, u32[]{:S(2)}, u32[]{:S(2)}) %collective-permute-start) | collective-permute-done | bytes 458784 | tf_op jit(solution)/shard_map/ppermute | solution.py:234
  34.5 0.0 collective-permute-done.1
  34.5 0.8 %add_convert_fusion = bf16[32,3584]{1,0:T(8,128)(2,1)} fusion(f32[32,3584]{1,0:T(8,128)S(1)} %collective-permute-done.1, f32[32,3584]{1,0:T(8,128)S(1)} %get-tuple-element.7, f32[32,3584]{1,0:T(8,128)S(1)} %collective-permute-done), kind=kLoop, calls=%fused_computation | loop fusion | flops 344064 | bytes 1605632 | tf_op jit(solution)/shard_map/convert_element_type | solution.py:239
Async XLA Ops:
  20.9 13.5 %collective-permute-start = (f32[32,3584]{1,0:T(8,128)S(1)}, f32[32,3584]{1,0:T(8,128)S(1)}, u32[]{:S(2)}, u32[]{:S(2)}) collective-permute-start(f32[32,3584]{1,0:T(8,128)S(1)} %get-tuple-element.8), channel_id=1, source_target_pairs={{2,4},{4,2},{3,5},{5,3},{6,0},{0,6},{7,1},{1,7},{10,12},{12,10},{1... | collective-permute-start | bytes 1376264 | tf_op jit(solution)/shard_map/ppermute | solution.py:234
  21.7 12.8 %collective-permute-start.1 = (f32[32,3584]{1,0:T(8,128)S(1)}, f32[32,3584]{1,0:T(8,128)S(1)}, u32[]{:S(2)}, u32[]{:S(2)}) collective-permute-start(f32[32,3584]{1,0:T(8,128)S(1)} %get-tuple-element.9), channel_id=1, source_target_pairs={{0,2},{2,0},{1,3},{3,1},{4,6},{6,4},{5,7},{7,5},{8,10},{10,8},{9,1... | collective-permute-start | bytes 1376264 | tf_op jit(solution)/shard_map/ppermute | solution.py:234

commit v10 on v9

--- a/solution.py
+++ b/solution.py
@@ -51,7 +51,7 @@
     own_x.start()
     g_load = pltpu.make_async_copy(gt_hbm, gt, g_sem)
     g_load.start()
-    ahead = 2
+    ahead = 3
 
     def w_load(j):
         cols = pl.ds(j * blk, blk)

time: 35.3 us -> 35.3 us (level)
  waiting for transfers between devices: 0.59 us -> 0.96 us
    ppermute x2, waiting for transfers between devices: 0.59 us -> 0.96 us  [swap(): return lax.ppermute(part, 'tp', pairs)]
where the time goes in v10:
time: 35.3 us; the launch traced here: 35.2 us
  Pallas kernels  31.4 us (89%)
  starting transfers between devices  1.51 us (4%)
  waiting for transfers between devices  0.96 us (3%)
  other arithmetic  0.76 us (2%)
  between operations  0.65 us (2%)
    pallas_call x1, Pallas kernels, exchange(): pl.pallas_call(functools.partial(exchange_kernel, n, groups), out_shape=(...  19.9 us
    pallas_call x1, Pallas kernels, weight_grad(): pl.pallas_call(weight_kernel, out_shape=jax.ShapeDtypeStruct((cols, width...  11.4 us
    ppermute x2, starting transfers between devices, swap(): return lax.ppermute(part, 'tp', pairs)  1.51 us
    ppermute x2, waiting for transfers between devices, swap(): return lax.ppermute(part, 'tp', pairs)  0.96 us
    convert_element_type x1, other arithmetic, per_device(): grad_x = (own + got_first + got_second).astype(BF16)  0.76 us
  transfers between devices with their start and end apart: 2, of which 1 were waited for; matrix products, arithmetic and copies ran while one was open for 0% of the time, Pallas kernels for 33%

profile of v10, /device:TPU:112, one launch (start us, length us, event | category | flops | bytes accessed | tf_op | source)
XLA Modules:
  0.0 35.2 jit_solution(14219767296289581180)
XLA Ops:
  0.6 19.9 %exchange.1 = (bf16[256,3584]{1,0:T(8,128)(2,1)S(1)}, bf16[2368,256]{1,0:T(8,128)(2,1)S(1)}, f32[32,3584]{1,0:T(8,128)S(1)}, f32[32,3584]{1,0:T(8,128)S(1)}, f32[32,3584]{1,0:T(8,128)S(1)}) custom-call(bf16[32,3584]{1,0:T(8,128)(2,1)} %x_hbm.1, bf16[2368,3584]{1,0:T(8,128)(2,1)} %bitcast.4, bf16[2368,256]{1,0:T(8,128)(2,1)} %bitcast.5), custom_call_target="tpu_custom_call" | custom-call | flops 4345298944 | bytes 16973824 | tf_op jit(solution)/shard_map/exchange/pallas_call | solution.py:158
  20.6 0.9 %collective-permute-start = (f32[32,3584]{1,0:T(8,128)S(1)}, f32[32,3584]{1,0:T(8,128)S(1)}, u32[]{:S(2)}, u32[]{:S(2)}) collective-permute-start(f32[32,3584]{1,0:T(8,128)S(1)} %get-tuple-element.8), channel_id=1, source_target_pairs={{2,4},{4,2},{3,5},{5,3},{6,0},{0,6},{7,1},{1,7},{10,12},{12,10},{1... | collective-permute-start | bytes 1376264 | tf_op jit(solution)/shard_map/ppermute | solution.py:234
  21.4 0.6 %collective-permute-start.1 = (f32[32,3584]{1,0:T(8,128)S(1)}, f32[32,3584]{1,0:T(8,128)S(1)}, u32[]{:S(2)}, u32[]{:S(2)}) collective-permute-start(f32[32,3584]{1,0:T(8,128)S(1)} %get-tuple-element.9), channel_id=1, source_target_pairs={{0,2},{2,0},{1,3},{3,1},{4,6},{6,4},{5,7},{7,5},{8,10},{10,8},{9,1... | collective-permute-start | bytes 1376264 | tf_op jit(solution)/shard_map/ppermute | solution.py:234
  22.1 11.4 %weight_grad.1 = f32[2368,3584]{1,0:T(8,128)} custom-call(bf16[256,3584]{1,0:T(8,128)(2,1)S(1)} %get-tuple-element.10.x, bf16[2368,256]{1,0:T(8,128)(2,1)S(1)} %get-tuple-element.11.gt), custom_call_target="tpu_custom_call" | custom-call | flops 4345298944 | bytes 33947648 | tf_op jit(solution)/shard_map/weight_grad/pallas_call | solution.py:209
  33.5 1.0 %collective-permute-done = f32[32,3584]{1,0:T(8,128)S(1)} collective-permute-done((f32[32,3584]{1,0:T(8,128)S(1)}, f32[32,3584]{1,0:T(8,128)S(1)}, u32[]{:S(2)}, u32[]{:S(2)}) %collective-permute-start) | collective-permute-done | bytes 458784 | tf_op jit(solution)/shard_map/ppermute | solution.py:234
  34.5 0.0 collective-permute-done.1
  34.5 0.8 %add_convert_fusion = bf16[32,3584]{1,0:T(8,128)(2,1)} fusion(f32[32,3584]{1,0:T(8,128)S(1)} %collective-permute-done.1, f32[32,3584]{1,0:T(8,128)S(1)} %get-tuple-element.7, f32[32,3584]{1,0:T(8,128)S(1)} %collective-permute-done), kind=kLoop, calls=%fused_computation | loop fusion | flops 344064 | bytes 1605632 | tf_op jit(solution)/shard_map/convert_element_type | solution.py:239
Async XLA Ops:
  20.6 13.9 %collective-permute-start = (f32[32,3584]{1,0:T(8,128)S(1)}, f32[32,3584]{1,0:T(8,128)S(1)}, u32[]{:S(2)}, u32[]{:S(2)}) collective-permute-start(f32[32,3584]{1,0:T(8,128)S(1)} %get-tuple-element.8), channel_id=1, source_target_pairs={{2,4},{4,2},{3,5},{5,3},{6,0},{0,6},{7,1},{1,7},{10,12},{12,10},{1... | collective-permute-start | bytes 1376264 | tf_op jit(solution)/shard_map/ppermute | solution.py:234
  21.4 13.1 %collective-permute-start.1 = (f32[32,3584]{1,0:T(8,128)S(1)}, f32[32,3584]{1,0:T(8,128)S(1)}, u32[]{:S(2)}, u32[]{:S(2)}) collective-permute-start(f32[32,3584]{1,0:T(8,128)S(1)} %get-tuple-element.9), channel_id=1, source_target_pairs={{0,2},{2,0},{1,3},{3,1},{4,6},{6,4},{5,7},{7,5},{8,10},{10,8},{9,1... | collective-permute-start | bytes 1376264 | tf_op jit(solution)/shard_map/ppermute | solution.py:234

commit v11 on v10

--- a/solution.py
+++ b/solution.py
@@ -70,17 +70,19 @@
 
     own_x.wait()
     ag = {}
-    ag[0] = send(at(me), at(me), ag_send.at[0], ag_recv.at[0], right)
-    ag[1] = send(at(me), at(me), ag_send.at[1], ag_recv.at[1], left)
+    ag[0] = send(low(me), low(me), ag_send.at[0], ag_recv.at[0], right)
+    ag[3] = send(high(me), high(me), ag_send.at[3], ag_recv.at[3], left)
+    ag[1] = send(high(me), high(me), ag_send.at[1], ag_recv.at[1], right)
+    ag[2] = send(low(me), low(me), ag_send.at[2], ag_recv.at[2], left)
     pr = {}
-    pr[4] = send(at(me), at(me), pr_send.at[4], pr_recv.at[4], peer)
+    pr[6] = send(at(me), at(me), pr_send.at[6], pr_recv.at[6], peer)
 
     def arrived(slot, block, onward=None):
         pltpu.make_async_remote_copy(src_ref=block, dst_ref=block, send_sem=ag_send.at[slot],
                                      recv_sem=ag_recv.at[slot], device_id={"tp": me}, device_id_type=MESH).wait_recv()
         if onward is not None:
-            to, piece, dev = onward
-            ag[to] = send(piece, piece, ag_send.at[to], ag_recv.at[to], dev)
+            to, dev = onward
+            ag[to] = send(block, block, ag_send.at[to], ag_recv.at[to], dev)
         pr[slot] = send(block, block, pr_send.at[slot], pr_recv.at[slot], peer)
 
     g_load.wait()
@@ -119,15 +121,17 @@
     partial(2)
     chip_sum(groups[0])
     partial(3)
+    arrived(0, low(left), (4, right))
+    arrived(3, high(right), (5, left))
     partial(4)
     chip_sum(groups[1])
     partial(5)
     partial(6)
-    arrived(0, at(left), (2, low(left), right))
-    arrived(1, at(right), (3, high(right), left))
+    arrived(1, high(left))
+    arrived(2, low(right))
     chip_sum(groups[2])
-    arrived(2, low(opp))
-    arrived(3, high(opp))
+    arrived(4, low(opp))
+    arrived(5, high(opp))
     for cp in pr.values():
         cp.wait()
     for cp in ag.values():
@@ -170,10 +174,10 @@
             pltpu.SemaphoreType.DMA,
             pltpu.SemaphoreType.DMA,
             pltpu.SemaphoreType.DMA((nb,)),
-            pltpu.SemaphoreType.DMA((4,)),
-            pltpu.SemaphoreType.DMA((4,)),
-            pltpu.SemaphoreType.DMA((5,)),
-            pltpu.SemaphoreType.DMA((5,)),
+            pltpu.SemaphoreType.DMA((6,)),
+            pltpu.SemaphoreType.DMA((6,)),
+            pltpu.SemaphoreType.DMA((7,)),
+            pltpu.SemaphoreType.DMA((7,)),
             pltpu.SemaphoreType.DMA((nb,)),
             pltpu.SemaphoreType.DMA((nb,)),
             pltpu.SemaphoreType.DMA((2, len(groups))),

time: 35.3 us -> 34.5 us (0.977)
  waiting for transfers between devices: 0.96 us -> 0.1 us
    ppermute x2, waiting for transfers between devices: 0.96 us -> 0.1 us  [swap(): return lax.ppermute(part, 'tp', pairs)]
where the time goes in v11:
time: 34.5 us; the launch traced here: 34.4 us
  Pallas kernels  31.4 us (91%)
  starting transfers between devices  1.49 us (4%)
  other arithmetic  0.76 us (2%)
  between operations  0.65 us (2%)
    pallas_call x1, Pallas kernels, exchange(): pl.pallas_call(functools.partial(exchange_kernel, n, groups), out_shape=(...  20 us
    pallas_call x1, Pallas kernels, weight_grad(): pl.pallas_call(weight_kernel, out_shape=jax.ShapeDtypeStruct((cols, width...  11.4 us
    ppermute x2, starting transfers between devices, swap(): return lax.ppermute(part, 'tp', pairs)  1.49 us
    convert_element_type x1, other arithmetic, per_device(): grad_x = (own + got_first + got_second).astype(BF16)  0.76 us
  transfers between devices with their start and end apart: 2, of which 1 were waited for; matrix products, arithmetic and copies ran while one was open for 0% of the time, Pallas kernels for 33%

profile of v11, /device:TPU:112, one launch (start us, length us, event | category | flops | bytes accessed | tf_op | source)
XLA Modules:
  0.0 34.4 jit_solution(2848579964377261058)
XLA Ops:
  0.6 20.0 %exchange.1 = (bf16[256,3584]{1,0:T(8,128)(2,1)S(1)}, bf16[2368,256]{1,0:T(8,128)(2,1)S(1)}, f32[32,3584]{1,0:T(8,128)S(1)}, f32[32,3584]{1,0:T(8,128)S(1)}, f32[32,3584]{1,0:T(8,128)S(1)}) custom-call(bf16[32,3584]{1,0:T(8,128)(2,1)} %x_hbm.1, bf16[2368,3584]{1,0:T(8,128)(2,1)} %bitcast.4, bf16[2368,256]{1,0:T(8,128)(2,1)} %bitcast.5), custom_call_target="tpu_custom_call" | custom-call | flops 4345298944 | bytes 16973824 | tf_op jit(solution)/shard_map/exchange/pallas_call | solution.py:162
  20.6 0.8 %collective-permute-start = (f32[32,3584]{1,0:T(8,128)S(1)}, f32[32,3584]{1,0:T(8,128)S(1)}, u32[]{:S(2)}, u32[]{:S(2)}) collective-permute-start(f32[32,3584]{1,0:T(8,128)S(1)} %get-tuple-element.8), channel_id=1, source_target_pairs={{2,4},{4,2},{3,5},{5,3},{6,0},{0,6},{7,1},{1,7},{10,12},{12,10},{1... | collective-permute-start | bytes 1376264 | tf_op jit(solution)/shard_map/ppermute | solution.py:238
  21.4 0.7 %collective-permute-start.1 = (f32[32,3584]{1,0:T(8,128)S(1)}, f32[32,3584]{1,0:T(8,128)S(1)}, u32[]{:S(2)}, u32[]{:S(2)}) collective-permute-start(f32[32,3584]{1,0:T(8,128)S(1)} %get-tuple-element.9), channel_id=1, source_target_pairs={{0,2},{2,0},{1,3},{3,1},{4,6},{6,4},{5,7},{7,5},{8,10},{10,8},{9,1... | collective-permute-start | bytes 1376264 | tf_op jit(solution)/shard_map/ppermute | solution.py:238
  22.1 11.4 %weight_grad.1 = f32[2368,3584]{1,0:T(8,128)} custom-call(bf16[256,3584]{1,0:T(8,128)(2,1)S(1)} %get-tuple-element.10.x, bf16[2368,256]{1,0:T(8,128)(2,1)S(1)} %get-tuple-element.11.gt), custom_call_target="tpu_custom_call" | custom-call | flops 4345298944 | bytes 33947648 | tf_op jit(solution)/shard_map/weight_grad/pallas_call | solution.py:213
  33.6 0.1 collective-permute-done
  33.7 0.0 collective-permute-done.1
  33.7 0.8 %add_convert_fusion = bf16[32,3584]{1,0:T(8,128)(2,1)} fusion(f32[32,3584]{1,0:T(8,128)S(1)} %collective-permute-done.1, f32[32,3584]{1,0:T(8,128)S(1)} %get-tuple-element.7, f32[32,3584]{1,0:T(8,128)S(1)} %collective-permute-done), kind=kLoop, calls=%fused_computation | loop fusion | flops 344064 | bytes 1605632 | tf_op jit(solution)/shard_map/convert_element_type | solution.py:243
Async XLA Ops:
  20.6 13.0 %collective-permute-start = (f32[32,3584]{1,0:T(8,128)S(1)}, f32[32,3584]{1,0:T(8,128)S(1)}, u32[]{:S(2)}, u32[]{:S(2)}) collective-permute-start(f32[32,3584]{1,0:T(8,128)S(1)} %get-tuple-element.8), channel_id=1, source_target_pairs={{2,4},{4,2},{3,5},{5,3},{6,0},{0,6},{7,1},{1,7},{10,12},{12,10},{1... | collective-permute-start | bytes 1376264 | tf_op jit(solution)/shard_map/ppermute | solution.py:238
  21.4 12.3 %collective-permute-start.1 = (f32[32,3584]{1,0:T(8,128)S(1)}, f32[32,3584]{1,0:T(8,128)S(1)}, u32[]{:S(2)}, u32[]{:S(2)}) collective-permute-start(f32[32,3584]{1,0:T(8,128)S(1)} %get-tuple-element.9), channel_id=1, source_target_pairs={{0,2},{2,0},{1,3},{3,1},{4,6},{6,4},{5,7},{7,5},{8,10},{10,8},{9,1... | collective-permute-start | bytes 1376264 | tf_op jit(solution)/shard_map/ppermute | solution.py:238

commit v12 on v11

--- a/solution.py
+++ b/solution.py
@@ -101,8 +101,6 @@
             part[j, c] = t[:, c]
         d2d[j] = send(part.at[j, 1 - core], rbuf.at[j], d_send.at[j], d_recv.at[j], peer)
 
-    u1 = []
-
     def chip_sum(js):
         for j in js:
             cols = pl.ds(j * blk, blk)
@@ -111,25 +109,47 @@
             own[:, cols] = part[j, core, chip] + rbuf[j, chip]
             first[:, cols] = part[j, core, c_first] + rbuf[j, c_first]
             second[:, cols] = part[j, core, c_second] + rbuf[j, c_second]
-        g0 = pl.ds(js[0], len(js))
-        k = len(u1)
-        u1.append((js, send(opp_sum.at[g0, lo], u1buf.at[g0, lo], u_send.at[0, k], u_recv.at[0, k], right),
-                   send(opp_sum.at[g0, hi], u1buf.at[g0, hi], u_send.at[1, k], u_recv.at[1, k], left)))
+
+    def group(k):
+        g0 = pl.ds(groups[k][0], len(groups[k]))
+        copies = [pltpu.make_async_remote_copy(src_ref=opp_sum.at[g0, side], dst_ref=u1buf.at[g0, side],
+                                               send_sem=u_send.at[i, k], recv_sem=u_recv.at[i, k],
+                                               device_id={"tp": dev}, device_id_type=MESH)
+                  for i, (side, dev) in enumerate(((lo, right), (hi, left)))]
+        return groups[k], *copies
+
+    def send_group(k):
+        for cp in group(k)[1:]:
+            cp.start()
+
 
     partial(0)
     partial(1)
     partial(2)
     chip_sum(groups[0])
+
+    @pl.when(core == 1)
+    def _():
+        send_group(0)
+
     partial(3)
     arrived(0, low(left), (4, right))
     arrived(3, high(right), (5, left))
+
+    @pl.when(core == 0)
+    def _():
+        send_group(0)
+
     partial(4)
     chip_sum(groups[1])
+    send_group(1)
     partial(5)
     partial(6)
     arrived(1, high(left))
     arrived(2, low(right))
     chip_sum(groups[2])
+    send_group(2)
+    u1 = [group(k) for k in range(len(groups))]
     arrived(4, low(opp))
     arrived(5, high(opp))
     for cp in pr.values():
@@ -193,7 +213,8 @@
 def weight_kernel(x, gt, o_hbm, obuf, o_sem):
     cols, width = o_hbm.shape
     blk = 256
-    pieces = [(0, blk, c, min(512, width - c)) for c in range(0, width, 512)]
+    cuts = [width // 7 * c for c in (0, 1, 3, 7)]
+    pieces = [(0, blk, a, b - a) for a, b in zip(cuts, cuts[1:])]
     pieces += [(r, min(blk, cols - r), 0, width) for r in range(blk, cols, blk)]
     stores = []
     for i, (r, nr, c, nc) in enumerate(pieces):

time: 34.5 us -> 35.2 us (1.020)
  waiting for transfers between devices: 0.1 us -> 0.6 us
    ppermute x2, waiting for transfers between devices: 0.1 us -> 0.6 us  [swap(): return lax.ppermute(part, 'tp', pairs)]
where the time goes in v12:
time: 35.2 us; the launch traced here: 35.1 us
  Pallas kernels  31.6 us (90%)
  starting transfers between devices  1.53 us (4%)
  other arithmetic  0.76 us (2%)
  between operations  0.65 us (2%)
  waiting for transfers between devices  0.6 us (2%)
    pallas_call x1, Pallas kernels, exchange(): pl.pallas_call(functools.partial(exchange_kernel, n, groups), out_shape=(...  20.1 us
    pallas_call x1, Pallas kernels, weight_grad(): pl.pallas_call(weight_kernel, out_shape=jax.ShapeDtypeStruct((cols, width...  11.4 us
    ppermute x2, starting transfers between devices, swap(): return lax.ppermute(part, 'tp', pairs)  1.53 us
    convert_element_type x1, other arithmetic, per_device(): grad_x = (own + got_first + got_second).astype(BF16)  0.76 us
  transfers between devices with their start and end apart: 2, of which 1 were waited for; matrix products, arithmetic and copies ran while one was open for 0% of the time, Pallas kernels for 33%

profile of v12, /device:TPU:112, one launch (start us, length us, event | category | flops | bytes accessed | tf_op | source)
XLA Modules:
  0.0 35.1 jit_solution(968025617015141516)
XLA Ops:
  0.6 20.1 %exchange.1 = (bf16[256,3584]{1,0:T(8,128)(2,1)S(1)}, bf16[2368,256]{1,0:T(8,128)(2,1)S(1)}, f32[32,3584]{1,0:T(8,128)S(1)}, f32[32,3584]{1,0:T(8,128)S(1)}, f32[32,3584]{1,0:T(8,128)S(1)}) custom-call(bf16[32,3584]{1,0:T(8,128)(2,1)} %x_hbm.1, bf16[2368,3584]{1,0:T(8,128)(2,1)} %bitcast.4, bf16[2368,256]{1,0:T(8,128)(2,1)} %bitcast.5), custom_call_target="tpu_custom_call" | custom-call | flops 4345298944 | bytes 16973824 | tf_op jit(solution)/shard_map/exchange/pallas_call | solution.py:182
  20.8 0.8 %collective-permute-start = (f32[32,3584]{1,0:T(8,128)S(1)}, f32[32,3584]{1,0:T(8,128)S(1)}, u32[]{:S(2)}, u32[]{:S(2)}) collective-permute-start(f32[32,3584]{1,0:T(8,128)S(1)} %get-tuple-element.8), channel_id=1, source_target_pairs={{2,4},{4,2},{3,5},{5,3},{6,0},{0,6},{7,1},{1,7},{10,12},{12,10},{1... | collective-permute-start | bytes 1376264 | tf_op jit(solution)/shard_map/ppermute | solution.py:259
  21.5 0.8 %collective-permute-start.1 = (f32[32,3584]{1,0:T(8,128)S(1)}, f32[32,3584]{1,0:T(8,128)S(1)}, u32[]{:S(2)}, u32[]{:S(2)}) collective-permute-start(f32[32,3584]{1,0:T(8,128)S(1)} %get-tuple-element.9), channel_id=1, source_target_pairs={{0,2},{2,0},{1,3},{3,1},{4,6},{6,4},{5,7},{7,5},{8,10},{10,8},{9,1... | collective-permute-start | bytes 1376264 | tf_op jit(solution)/shard_map/ppermute | solution.py:259
  22.3 11.4 %weight_grad.1 = f32[2368,3584]{1,0:T(8,128)} custom-call(bf16[256,3584]{1,0:T(8,128)(2,1)S(1)} %get-tuple-element.10.x, bf16[2368,256]{1,0:T(8,128)(2,1)S(1)} %get-tuple-element.11.gt), custom_call_target="tpu_custom_call" | custom-call | flops 4345298944 | bytes 33947648 | tf_op jit(solution)/shard_map/weight_grad/pallas_call | solution.py:234
  33.8 0.6 %collective-permute-done = f32[32,3584]{1,0:T(8,128)S(1)} collective-permute-done((f32[32,3584]{1,0:T(8,128)S(1)}, f32[32,3584]{1,0:T(8,128)S(1)}, u32[]{:S(2)}, u32[]{:S(2)}) %collective-permute-start) | collective-permute-done | bytes 458784 | tf_op jit(solution)/shard_map/ppermute | solution.py:259
  34.4 0.0 collective-permute-done.1
  34.4 0.8 %add_convert_fusion = bf16[32,3584]{1,0:T(8,128)(2,1)} fusion(f32[32,3584]{1,0:T(8,128)S(1)} %collective-permute-done.1, f32[32,3584]{1,0:T(8,128)S(1)} %get-tuple-element.7, f32[32,3584]{1,0:T(8,128)S(1)} %collective-permute-done), kind=kLoop, calls=%fused_computation | loop fusion | flops 344064 | bytes 1605632 | tf_op jit(solution)/shard_map/convert_element_type | solution.py:264
Async XLA Ops:
  20.8 13.6 %collective-permute-start = (f32[32,3584]{1,0:T(8,128)S(1)}, f32[32,3584]{1,0:T(8,128)S(1)}, u32[]{:S(2)}, u32[]{:S(2)}) collective-permute-start(f32[32,3584]{1,0:T(8,128)S(1)} %get-tuple-element.8), channel_id=1, source_target_pairs={{2,4},{4,2},{3,5},{5,3},{6,0},{0,6},{7,1},{1,7},{10,12},{12,10},{1... | collective-permute-start | bytes 1376264 | tf_op jit(solution)/shard_map/ppermute | solution.py:259
  21.5 12.8 %collective-permute-start.1 = (f32[32,3584]{1,0:T(8,128)S(1)}, f32[32,3584]{1,0:T(8,128)S(1)}, u32[]{:S(2)}, u32[]{:S(2)}) collective-permute-start(f32[32,3584]{1,0:T(8,128)S(1)} %get-tuple-element.9), channel_id=1, source_target_pairs={{0,2},{2,0},{1,3},{3,1},{4,6},{6,4},{5,7},{7,5},{8,10},{10,8},{9,1... | collective-permute-start | bytes 1376264 | tf_op jit(solution)/shard_map/ppermute | solution.py:259

commit v13 on v11

--- a/solution.py
+++ b/solution.py
@@ -130,8 +130,20 @@
     arrived(1, high(left))
     arrived(2, low(right))
     chip_sum(groups[2])
+
+    def finish(entry):
+        js, from_left, from_right = entry
+        from_left.wait_recv()
+        from_right.wait_recv()
+        for j in js:
+            cols = pl.ds(j * blk, blk)
+            first[pl.ds(r_first, half), cols] += u1buf[j, pl.ds(r_first, half)]
+            second[pl.ds(r_second, half), cols] += u1buf[j, pl.ds(r_second, half)]
+
+    finish(u1[0])
     arrived(4, low(opp))
     arrived(5, high(opp))
+    finish(u1[1])
     for cp in pr.values():
         cp.wait()
     for cp in ag.values():
@@ -141,13 +153,7 @@
     for _, a, b in u1:
         a.wait_send()
         b.wait_send()
-    for js, from_left, from_right in u1:
-        from_left.wait_recv()
-        from_right.wait_recv()
-        for j in js:
-            cols = pl.ds(j * blk, blk)
-            first[pl.ds(r_first, half), cols] += u1buf[j, pl.ds(r_first, half)]
-            second[pl.ds(r_second, half), cols] += u1buf[j, pl.ds(r_second, half)]
+    finish(u1[2])
 
 
 def exchange(x_blk, wt_blk, gt_blk, n):

time: 34.5 us -> 34.5 us (level)
  no operation moved by 1% of the time
where the time goes in v13:
time: 34.5 us; the launch traced here: 34.4 us
  Pallas kernels  31.4 us (91%)
  starting transfers between devices  1.49 us (4%)
  other arithmetic  0.76 us (2%)
  between operations  0.65 us (2%)
    pallas_call x1, Pallas kernels, exchange(): pl.pallas_call(functools.partial(exchange_kernel, n, groups), out_shape=(...  20 us
    pallas_call x1, Pallas kernels, weight_grad(): pl.pallas_call(weight_kernel, out_shape=jax.ShapeDtypeStruct((cols, width...  11.4 us
    ppermute x2, starting transfers between devices, swap(): return lax.ppermute(part, 'tp', pairs)  1.49 us
    convert_element_type x1, other arithmetic, per_device(): grad_x = (own + got_first + got_second).astype(BF16)  0.76 us
  transfers between devices with their start and end apart: 2, of which 1 were waited for; matrix products, arithmetic and copies ran while one was open for 0% of the time, Pallas kernels for 33%

profile of v13, /device:TPU:112, one launch (start us, length us, event | category | flops | bytes accessed | tf_op | source)
XLA Modules:
  0.0 34.4 jit_solution(5167140788407151242)
XLA Ops:
  0.6 20.0 %exchange.1 = (bf16[256,3584]{1,0:T(8,128)(2,1)S(1)}, bf16[2368,256]{1,0:T(8,128)(2,1)S(1)}, f32[32,3584]{1,0:T(8,128)S(1)}, f32[32,3584]{1,0:T(8,128)S(1)}, f32[32,3584]{1,0:T(8,128)S(1)}) custom-call(bf16[32,3584]{1,0:T(8,128)(2,1)} %x_hbm.1, bf16[2368,3584]{1,0:T(8,128)(2,1)} %bitcast.4, bf16[2368,256]{1,0:T(8,128)(2,1)} %bitcast.5), custom_call_target="tpu_custom_call" | custom-call | flops 4345298944 | bytes 16973824 | tf_op jit(solution)/shard_map/exchange/pallas_call | solution.py:168
  20.6 0.8 %collective-permute-start = (f32[32,3584]{1,0:T(8,128)S(1)}, f32[32,3584]{1,0:T(8,128)S(1)}, u32[]{:S(2)}, u32[]{:S(2)}) collective-permute-start(f32[32,3584]{1,0:T(8,128)S(1)} %get-tuple-element.8), channel_id=1, source_target_pairs={{2,4},{4,2},{3,5},{5,3},{6,0},{0,6},{7,1},{1,7},{10,12},{12,10},{1... | collective-permute-start | bytes 1376264 | tf_op jit(solution)/shard_map/ppermute | solution.py:244
  21.4 0.7 %collective-permute-start.1 = (f32[32,3584]{1,0:T(8,128)S(1)}, f32[32,3584]{1,0:T(8,128)S(1)}, u32[]{:S(2)}, u32[]{:S(2)}) collective-permute-start(f32[32,3584]{1,0:T(8,128)S(1)} %get-tuple-element.9), channel_id=1, source_target_pairs={{0,2},{2,0},{1,3},{3,1},{4,6},{6,4},{5,7},{7,5},{8,10},{10,8},{9,1... | collective-permute-start | bytes 1376264 | tf_op jit(solution)/shard_map/ppermute | solution.py:244
  22.1 11.4 %weight_grad.1 = f32[2368,3584]{1,0:T(8,128)} custom-call(bf16[256,3584]{1,0:T(8,128)(2,1)S(1)} %get-tuple-element.10.x, bf16[2368,256]{1,0:T(8,128)(2,1)S(1)} %get-tuple-element.11.gt), custom_call_target="tpu_custom_call" | custom-call | flops 4345298944 | bytes 33947648 | tf_op jit(solution)/shard_map/weight_grad/pallas_call | solution.py:219
  33.6 0.1 collective-permute-done
  33.7 0.0 collective-permute-done.1
  33.7 0.8 %add_convert_fusion = bf16[32,3584]{1,0:T(8,128)(2,1)} fusion(f32[32,3584]{1,0:T(8,128)S(1)} %collective-permute-done.1, f32[32,3584]{1,0:T(8,128)S(1)} %get-tuple-element.7, f32[32,3584]{1,0:T(8,128)S(1)} %collective-permute-done), kind=kLoop, calls=%fused_computation | loop fusion | flops 344064 | bytes 1605632 | tf_op jit(solution)/shard_map/convert_element_type | solution.py:249
Async XLA Ops:
  20.6 13.0 %collective-permute-start = (f32[32,3584]{1,0:T(8,128)S(1)}, f32[32,3584]{1,0:T(8,128)S(1)}, u32[]{:S(2)}, u32[]{:S(2)}) collective-permute-start(f32[32,3584]{1,0:T(8,128)S(1)} %get-tuple-element.8), channel_id=1, source_target_pairs={{2,4},{4,2},{3,5},{5,3},{6,0},{0,6},{7,1},{1,7},{10,12},{12,10},{1... | collective-permute-start | bytes 1376264 | tf_op jit(solution)/shard_map/ppermute | solution.py:244
  21.4 12.3 %collective-permute-start.1 = (f32[32,3584]{1,0:T(8,128)S(1)}, f32[32,3584]{1,0:T(8,128)S(1)}, u32[]{:S(2)}, u32[]{:S(2)}) collective-permute-start(f32[32,3584]{1,0:T(8,128)S(1)} %get-tuple-element.9), channel_id=1, source_target_pairs={{0,2},{2,0},{1,3},{3,1},{4,6},{6,4},{5,7},{7,5},{8,10},{10,8},{9,1... | collective-permute-start | bytes 1376264 | tf_op jit(solution)/shard_map/ppermute | solution.py:244
